TPU v7x, 128 devices: a whole 4x4x4 slice. The times are simulated.
128 devices in a mesh: dom: 8 (over z, core), feat: 16 (over x, y).
Axes of the slice: x: 4, y: 4, z: 4, core: 2. Of those that a mesh axis runs over, the one named last changes fastest.
Arguments:
- node_feats: bfloat16 [8192, 512], P('dom', 'feat'), may hold values from -6 to 6
- rel_weight: bfloat16 [4, 512, 512], replicated, may hold values from -0.25 to 0.25
- self_weight: bfloat16 [512, 512], replicated, may hold values from -0.25 to 0.25
- bias: float32 [512], replicated, may hold values from -3 to 3
- out_degree: int32 [4, 8192], P(None, 'dom'), may hold values from 0 to 63
- adjacency: int32 [8, 16, 64, 256, 256], P('dom', 'feat'), may hold values 0 or 1
- tile_index: int32 [8, 16, 64, 3], P('dom', 'feat'), may hold values from 0 to 31, as said below
- tile_count: int32 [8, 16], P('dom', 'feat'), may hold values from 1 to 64, as said below
Outputs:
- embedding: bfloat16 [8192, 512], P('dom', 'feat')
Inputs may be any that keep to these rules, and one draw needn't show every extreme that they name: `tile_index`: the three entries of a slot are a relation below 4, a destination block below 32 and a source block of the device's own group below 4; entries of slots beyond a device's count are arbitrary within the range. `tile_count`: some device holds exactly 64 live slots.
All inputs are finite; a program needn't handle non-finite values. No bound on the sum of `adjacency` on one device may be relied on, other than what follows from the above.
Results may differ from a plain program's by a relative error of at most 0.0049.
Values may be sent and summed in bfloat16 or wider, within the bound.
A program may use at most 128 MiB of HBM per device.

v0:
```python
import jax
import jax.numpy as jnp
from jax import lax
from jax.sharding import PartitionSpec as P


def copy_for_each(value, axis):
    copies = jnp.broadcast_to(value, (lax.axis_size(axis), *value.shape))
    return lax.all_to_all(copies, axis, split_axis=0, concat_axis=0, tiled=True)


def joined_along(tiles, dim):
    shape = list(tiles.shape[1:])
    shape[dim] *= tiles.shape[0]
    return jnp.moveaxis(tiles, 0, dim).reshape(shape)


def gathered_copies(value, axis, dim):
    tiles = copy_for_each(value, axis)
    return joined_along(tiles, dim)


def cut_along(value, dim, devices):
    before, after = (value.shape[:dim], value.shape[dim + 1 :])
    return jnp.moveaxis(value.reshape(*before, devices, -1, *after), dim, 0)


def sum_at_owner(value, axis, dim):
    tiles = cut_along(value, dim, lax.axis_size(axis))
    arrived = lax.all_to_all(tiles, axis, split_axis=0, concat_axis=0, tiled=True)
    return arrived.sum(axis=0)


def body(node_feats, rel_weight, self_weight, bias, out_degree, adjacency, tile_index, tile_count):
    owned_nodes = node_feats.shape[0]
    column_count = node_feats.shape[1]
    hidden_width = rel_weight.shape[1]
    tile_size = adjacency.shape[-1]
    group_count = lax.axis_size("dom")
    column_start = lax.axis_index("feat") * column_count
    features = gathered_copies(node_feats, "feat", 1)
    inv_degree = 1.0 / jnp.maximum(out_degree, 1).astype(jnp.float32)
    adjacency_tiles = adjacency[0, 0]
    tile_list = tile_index[0, 0]
    live_tiles = tile_count[0, 0]
    self_columns = lax.dynamic_slice_in_dim(self_weight, column_start, column_count, 1)
    bias_columns = lax.dynamic_slice_in_dim(bias, column_start, column_count, 0)
    self_term = (
        jnp.dot(features, self_columns, preferred_element_type=jnp.float32) + bias_columns[None, :]
    )

    def source_rows(relation, source):
        source_block = lax.dynamic_slice_in_dim(features, source * tile_size, tile_size, 0)
        relation_matrix = lax.dynamic_index_in_dim(rel_weight, relation, 0, keepdims=False)
        degree_factor = lax.dynamic_slice(
            inv_degree, (relation, source * tile_size), (1, tile_size)
        )[0]
        product = jnp.dot(source_block, relation_matrix, preferred_element_type=jnp.float32)
        return (product * degree_factor[:, None]).astype(jnp.bfloat16)

    def add_tile(slot_index, running):
        relation = tile_list[slot_index, 0]
        target = tile_list[slot_index, 1]
        source = tile_list[slot_index, 2]
        source_msg = source_rows(relation, source)
        tile_cells = lax.dynamic_index_in_dim(adjacency_tiles, slot_index, 0, keepdims=False)
        contribution = jnp.dot(
            tile_cells.astype(jnp.bfloat16), source_msg, preferred_element_type=jnp.float32
        )
        current = lax.dynamic_slice_in_dim(running, target * tile_size, tile_size, 0)
        return lax.dynamic_update_slice_in_dim(
            running, current + contribution, target * tile_size, 0
        )

    partial_value = jnp.zeros((group_count * owned_nodes, hidden_width), jnp.float32)
    partial_value = lax.fori_loop(0, live_tiles, add_tile, partial_value)
    owned_sums = lax.psum_scatter(partial_value, "dom", scatter_dimension=0, tiled=True)
    reduced = sum_at_owner(owned_sums, "feat", 1)
    return (reduced + self_term).astype(jnp.bfloat16)


def solution(mesh):
    placed = (
        P("dom", "feat"),
        P(),
        P(),
        P(),
        P(None, "dom"),
        P("dom", "feat", None, None, None),
        P("dom", "feat", None, None),
        P("dom", "feat"),
    )
    return jax.shard_map(
        body, mesh=mesh, in_specs=placed, out_specs=P("dom", "feat"), check_vma=False
    )
```

profile of v0, /device:TPU:0, one launch (start us, length us, event | category | flops | bytes accessed | tf_op | source)
XLA Modules:
  0.0 729.4 jit_solution(5827715958033985486)
XLA Ops:
  6.5 2.0 broadcast_in_dim.8
  8.5 7.1 all-to-all-start
  17.1 16.3 %all-to-all-done = bf16[16,1024,32]{1,2,0:T(8,128)(2,1)S(1)} async-done(((bf16[16,1024,32]{1,2,0:T(8,128)(2,1)}), bf16[16,1024,32]{1,2,0:T(8,128)(2,1)S(1)}, u32[]{:S(2)}, u32[]{:S(2)}) %all-to-all-start) | async-done | bytes 1048608 | tf_op jit(solution)/shard_map/all_to_all | solution.py:9
  33.4 7.8 %broadcast_in_dim.7.clone = f32[8192,512]{0,1:T(8,128)} broadcast(f32[]{:T(128)} %constant.9.clone.1), dimensions={} | broadcast | bytes 16777220 | tf_op jit(solution)/shard_map/broadcast_in_dim | solution.py:75
  41.2 556.0 %while.10 = (s32[]{:T(128)}, f32[8192,512]{0,1:T(8,128)}, s32[]{:T(128)}, s32[64,3]{0,1:T(4,128)S(1)}, s32[64,256,256]{2,1,0:T(8,128)}, /*index=5*/bf16[1024,512...) while((s32[]{:T(128)}, f32[8192,512]{0,1:T(8,128)}, ...), condition=%wide.region_1.2_spmd, body=%wide.region_0.1_spmd.sunk | while | flops 201785360 | bytes 6294889 | solution.py:76
  55.8 1.7 convolution_add_fusion.3
  64.5 1.7 convolution_add_fusion.3
  81.9 1.7 convolution_add_fusion.3
  107.9 1.7 convolution_add_fusion.3
  125.3 1.7 convolution_add_fusion.3
  142.6 1.7 convolution_add_fusion.3
  160.0 1.7 convolution_add_fusion.3
  168.6 1.7 convolution_add_fusion.3
  177.3 1.7 convolution_add_fusion.3
  194.7 1.7 convolution_add_fusion.3
  203.3 1.7 convolution_add_fusion.3
  220.7 1.7 convolution_add_fusion.3
  255.4 1.7 convolution_add_fusion.3
  264.1 1.7 convolution_add_fusion.3
  281.4 1.7 convolution_add_fusion.3
  290.1 1.7 convolution_add_fusion.3
  307.5 1.7 convolution_add_fusion.3
  316.2 1.7 convolution_add_fusion.3
  324.8 1.7 convolution_add_fusion.3
  333.5 1.7 convolution_add_fusion.3
  342.2 1.7 convolution_add_fusion.3
  350.9 1.7 convolution_add_fusion.3
  368.2 1.7 convolution_add_fusion.3
  376.9 1.7 convolution_add_fusion.3
  385.6 1.7 convolution_add_fusion.3
  402.9 1.7 convolution_add_fusion.3
  411.6 1.7 convolution_add_fusion.3
  420.3 1.7 convolution_add_fusion.3
  429.0 1.7 convolution_add_fusion.3
  463.7 1.7 convolution_add_fusion.3
  489.8 1.7 convolution_add_fusion.3
  498.4 1.7 convolution_add_fusion.3
  515.8 1.7 convolution_add_fusion.3
  524.5 1.7 convolution_add_fusion.3
  533.1 1.7 convolution_add_fusion.3
  541.8 1.7 convolution_add_fusion.3
  576.5 1.7 convolution_add_fusion.3
  585.2 1.7 convolution_add_fusion.3
  593.9 1.7 convolution_add_fusion.3
  597.3 86.5 %reduce-scatter.2.cloned.1.call-done = f32[1024,512]{0,1:T(8,128)} async-done(((f32[8192,512]{0,1:T(8,128)}), f32[1024,512]{0,1:T(8,128)}) %reduce-scatter.2.cloned.1.call-update) | async-done | bytes 2097168 | tf_op jit(solution)/shard_map/reduce_scatter | solution.py:77
  683.8 6.9 all-to-all-start.1
  691.4 28.3 %all-to-all-done.1 = f32[16,1024,32]{1,2,0:T(8,128)} async-done(((f32[16,1024,32]{1,2,0:T(8,128)}), f32[16,1024,32]{1,2,0:T(8,128)}, u32[]{:S(2)}, u32[]{:S(2)}) %all-to-all-start.1) | async-done | bytes 2097184 | tf_op jit(solution)/shard_map/all_to_all | solution.py:30
  719.8 1.7 reduce_sum.9
  (417 shorter events, 241.4 us)
Async XLA Ops:
  6.5 715.0 %copy-start = (bf16[512,512]{1,0:T(8,128)(2,1)S(1)}, bf16[512,512]{1,0:T(8,128)(2,1)}, u32[]{:S(2)}) copy-start(bf16[512,512]{1,0:T(8,128)(2,1)} %param.12) | copy-start | bytes 1572868
  8.5 24.9 %all-to-all-start = ((bf16[16,1024,32]{1,2,0:T(8,128)(2,1)}), bf16[16,1024,32]{1,2,0:T(8,128)(2,1)S(1)}, u32[]{:S(2)}, u32[]{:S(2)}) async-start(bf16[16,1024,32]{1,2,0:T(8,128)(2,1)} %broadcast_in_dim.8), calls=%async_computation | async-start | bytes 2097152 | tf_op jit(solution)/shard_map/all_to_all | solution.py:9
  15.7 668.1 %reduce-scatter.2.cloned.1.call-start = ((), (), s32[]{:S(2)}) async-start(), calls=%async_computation.3 | async-start | bytes 18874368 | tf_op jit(solution)/shard_map/reduce_scatter | solution.py:77
  683.8 36.0 %all-to-all-start.1 = ((f32[16,1024,32]{1,2,0:T(8,128)}), f32[16,1024,32]{1,2,0:T(8,128)}, u32[]{:S(2)}, u32[]{:S(2)}) async-start(f32[16,1024,32]{1,2,0:T(8,128)} %bitcast.42), calls=%async_computation.2 | async-start | bytes 4194304 | tf_op jit(solution)/shard_map/all_to_all | solution.py:30
Sparse Core Ops, SparseCore 0:
  597.4 86.3 reduce-scatter.1
where the time goes:
time: 739 us; the launch traced here: 729 us
  loops' own time  253 us (34%)
  local copies, waits for them, and re-layouts  208 us (28%)
  waiting for transfers between devices  131 us (18%)
  matrix products  107 us (14%)
  starting transfers between devices  14.1 us (2%)
  between operations  13.4 us (2%)
    another operation x1, loops' own time, body(): partial_value = lax.fori_loop(0, live_tiles, add_tile, partial_value)  253 us
    dot_general x64, matrix products, add_tile(): jnp.dot(tile_cells.astype(jnp.bfloat16), source_msg, preferred_element_ty...  106 us
    reduce_scatter x1, waiting for transfers between devices, body(): lax.psum_scatter(partial_value, 'dom', scatter_dimension=0, tiled=True)  86.5 us
    dynamic_slice x128, local copies, waits for them, and re-layouts, add_tile(): lax.dynamic_slice_in_dim(running, target * tile_size, tile_size, 0)  81.8 us
    dynamic_update_slice x128, local copies, waits for them, and re-layouts, add_tile(): lax.dynamic_update_slice_in_dim(running, current + contribution, target *...  67.4 us
    dynamic_slice x64, local copies, waits for them, and re-layouts, add_tile(): source = tile_list[slot_index, 2]  42.5 us
    all_to_all x1, waiting for transfers between devices, sum_at_owner(): lax.all_to_all(tiles, axis, split_axis=0, concat_axis=0, tiled=True)  28.3 us
    all_to_all x1, waiting for transfers between devices, copy_for_each(): return lax.all_to_all(copies, axis, split_axis=0, concat_axis=0, tiled=True)  16.3 us
  transfers between devices with their start and end apart: 3, of which 3 were waited for; matrix products, arithmetic and copies ran while one was open for 0% of the time, Pallas kernels for 0%

commit v1 on v0

v1 whole, which is shorter than its diff:
```python
import functools

import jax
import jax.numpy as jnp
from jax import lax
from jax.experimental import pallas as pl
from jax.experimental.pallas import tpu as pltpu
from jax.sharding import PartitionSpec as P

MESH = pl.DeviceIdType.MESH
BF = jnp.bfloat16
F32 = jnp.float32
RING = 4
HID = 512
COLS = 32
OWN = 1024
TILE = 256
SLOTS = 64
REL = 4
GROUPS = 8
BLOCKS = 32
LANES = (384, 384, 256)
VMEM = pl.BlockSpec(memory_space=pltpu.VMEM)
SMEM = pl.BlockSpec(memory_space=pltpu.SMEM)
HBM = pl.BlockSpec(memory_space=pl.ANY)
NT = (((1,), (1,)), ((), ()))


def place():
    dom = lax.axis_index("dom")
    feat = lax.axis_index("feat")
    return dict(z=dom // 2, c=dom % 2, x=feat // RING, y=feat % RING)


def device(here, **moved):
    at = dict(here)
    for axis, step in moved.items():
        at[axis] = (at[axis] + step) % (2 if axis == "c" else RING)
    return (at["z"] * 2 + at["c"], at["x"] * RING + at["y"])


def greet(peers):
    barrier = pltpu.get_barrier_semaphore()
    for peer in peers:
        pl.semaphore_signal(barrier, inc=1, device_id=peer, device_id_type=MESH)
    pl.semaphore_wait(barrier, len(peers))


def messages_kernel(
    nodes, rel, own, bias, degree, msg, self_term,
    feats, rel_in, own_in, rel_t, own_t, bias_t, send, recv, local,
):
    here = place()
    fetch_rel = pltpu.make_async_copy(rel, rel_in, local.at[0])
    fetch_own = pltpu.make_async_copy(own, own_in, local.at[1])
    fetch_rel.start()
    fetch_own.start()
    peers = [device(here, **{axis: step}) for axis in "xy" for step in (1, 2, 3)]
    greet(peers)
    half = COLS // 2
    first_axis = ("x", "y")
    second_axis = ("y", "x")

    def rows(h, x, y):
        return pl.ds(pl.multiple_of((x * RING + y) * COLS + h * half, half), half)

    def chunk(h, a, b):
        moved = {first_axis[h]: a, second_axis[h]: b}
        return rows(h, (here["x"] + moved["x"]) % RING, (here["y"] + moved["y"]) % RING)

    count = [0]
    started = []

    def remote(src, dst, peer):
        i = count[0]
        count[0] += 1
        copy = pltpu.make_async_remote_copy(
            src_ref=src, dst_ref=dst, send_sem=send.at[i], recv_sem=recv.at[i],
            device_id=peer, device_id_type=MESH,
        )
        return copy

    feats[rows(0, here["x"], here["y"]), :] = nodes[pl.ds(0, half), :]
    feats[rows(1, here["x"], here["y"]), :] = nodes[pl.ds(half, half), :]
    first = {}
    second = {}
    relay = {}
    left = pl.ds(0, OWN // 2)
    right = pl.ds(OWN // 2, OWN // 2)

    def part(h, a, b, lanes=None):
        at = chunk(h, a, b)
        return feats.at[at, :] if lanes is None else feats.at[at, lanes]

    for h in (0, 1):
        for step in (1, 3, 2):
            src = nodes.at[pl.ds(h * half, half), :]
            first[h, step] = remote(src, part(h, 0, 0), device(here, **{first_axis[h]: step}))
        for step in (1, 3):
            src = nodes.at[pl.ds(h * half, half), :]
            second[h, 0, step] = remote(src, part(h, 0, 0), device(here, **{second_axis[h]: step}))
        for a in (1, 3, 2):
            for step in (1, 3):
                second[h, a, step] = remote(
                    part(h, a, 0), part(h, a, 0), device(here, **{second_axis[h]: step})
                )
        for a in (0, 1, 3, 2):
            relay[h, a, 1] = remote(
                part(h, a, 3, left), part(h, a, 3, left), device(here, **{second_axis[h]: 1})
            )
            relay[h, a, 3] = remote(
                part(h, a, 1, right), part(h, a, 1, right), device(here, **{second_axis[h]: 3})
            )
    for step in (1, 3, 2):
        for h in (0, 1):
            first[h, step].start()
    for step in (1, 3):
        for h in (0, 1):
            second[h, 0, step].start()

    fetch_rel.wait()
    fetch_own.wait()
    rel_t[0] = rel_in[0].T
    for a in (3, 1):
        for h in (0, 1):
            first[h, RING - a].wait_recv()
            second[h, a, 1].start()
            second[h, a, 3].start()
    rel_t[1] = rel_in[1].T
    for h in (0, 1):
        second[h, 0, 1].wait_recv()
        relay[h, 0, 1].start()
        second[h, 0, 3].wait_recv()
        relay[h, 0, 3].start()
    for h in (0, 1):
        first[h, 2].wait_recv()
        second[h, 2, 1].start()
        second[h, 2, 3].start()
    rel_t[2] = rel_in[2].T
    for a in (3, 1):
        for h in (0, 1):
            second[h, a, 1].wait_recv()
            relay[h, a, 1].start()
            second[h, a, 3].wait_recv()
            relay[h, a, 3].start()
    rel_t[3] = rel_in[3].T
    for h in (0, 1):
        second[h, 2, 1].wait_recv()
        relay[h, 2, 1].start()
        second[h, 2, 3].wait_recv()
        relay[h, 2, 3].start()
    own_t[...] = own_in[...].T
    bias_t[...] = jnp.broadcast_to(bias[...], (128, HID)).T
    for a in (0, 3, 1, 2):
        for h in (0, 1):
            relay[h, a, 1].wait_recv()
            relay[h, a, 3].wait_recv()

    mine = pl.ds(pl.multiple_of((here["x"] * RING + here["y"]) * COLS, COLS), COLS)
    own_rows = own_t[mine, :]
    bias_rows = bias_t[mine, :]
    for s in range(OWN // TILE):
        at = pl.ds(s * TILE, TILE)
        block = feats[:, at]
        self_term[:, at] = (
            jnp.dot(own_rows, block, preferred_element_type=F32)
            + jnp.concatenate([bias_rows, bias_rows], axis=1)
        )

        def relation(r, carry):
            product = jnp.dot(rel_t[r], block, preferred_element_type=F32)
            factor = 1.0 / jnp.maximum(degree[pl.ds(r, 1), at], 1).astype(F32)
            msg[r * 4 + s] = (product * factor).astype(BF)
            return carry

        lax.fori_loop(0, REL, relation, 0)
    for copies in (first, second, relay):
        for copy in copies.values():
            copy.wait_send()


def messages(nodes, rel, own, bias, degree):
    copies = 2 * (3 + 8 + 8)
    return pl.pallas_call(
        messages_kernel,
        out_shape=(
            jax.ShapeDtypeStruct((REL * 4, HID, TILE), BF),
            jax.ShapeDtypeStruct((COLS, OWN), F32),
        ),
        in_specs=[VMEM, HBM, HBM, VMEM, VMEM],
        out_specs=(VMEM, VMEM),
        scratch_shapes=[
            pltpu.VMEM((HID, OWN), BF),
            pltpu.VMEM((REL, HID, HID), BF),
            pltpu.VMEM((HID, HID), BF),
            pltpu.VMEM((REL, HID, HID), BF),
            pltpu.VMEM((HID, HID), BF),
            pltpu.VMEM((HID, 128), F32),
            pltpu.SemaphoreType.DMA((copies,)),
            pltpu.SemaphoreType.DMA((copies,)),
            pltpu.SemaphoreType.DMA((2,)),
        ],
        compiler_params=pltpu.CompilerParams(collective_id=0, has_side_effects=True),
        name="messages",
    )(nodes, rel, own, bias, degree)


def tiles_kernel(index, live, msg, tiles, part_x, part_y, part_z, cells, total, arrived):
    parts = (part_x, part_y, part_z)
    count = live[0]

    def fetch(k):
        return pltpu.make_async_copy(tiles.at[k], cells.at[k], arrived.at[k])

    def start(k, carry):
        fetch(k).start()
        return carry

    lax.fori_loop(0, count, start, 0)

    def clear(d, carry):
        total[d] = jnp.zeros((HID, TILE), F32)
        return carry

    lax.fori_loop(0, BLOCKS, clear, 0)

    def add(k, carry):
        relation = index[0, k]
        target = index[1, k]
        source = index[2, k]
        fetch(k).wait()
        total[target] += lax.dot_general(
            msg[relation * 4 + source], cells[k].astype(F32).astype(BF), NT, preferred_element_type=F32
        )
        return carry

    lax.fori_loop(0, count, add, 0)

    def store(i, carry):
        f = i % 16
        g = i // 16
        x, y = f // RING, f % RING
        z, c = g // 2, g % 2
        at = pl.ds(pl.multiple_of(f * COLS, COLS), COLS)
        block = [total[g * 4 + b, at, :].astype(BF) for b in range(4)]
        part_x[c, x, y, z, :, 0:256] = block[0]
        part_x[c, x, y, z, :, 256:384] = block[1][:, 0:128]
        part_y[c, y, z, x, :, 0:128] = block[1][:, 128:256]
        part_y[c, y, z, x, :, 128:384] = block[2]
        part_z[c, z, x, y, :, :] = block[3]
        return carry

    lax.fori_loop(0, GROUPS * 16, store, 0)


def tile_sums(index, live, msg, tiles):
    return pl.pallas_call(
        tiles_kernel,
        out_shape=tuple(
            jax.ShapeDtypeStruct((2, RING, RING, RING, COLS, lanes), BF) for lanes in LANES
        ),
        in_specs=[SMEM, SMEM, VMEM, HBM],
        out_specs=(VMEM,) * 3,
        scratch_shapes=[
            pltpu.VMEM((SLOTS, TILE, TILE), jnp.int32),
            pltpu.VMEM((BLOCKS, HID, TILE), F32),
            pltpu.SemaphoreType.DMA((SLOTS,)),
        ],
        compiler_params=pltpu.CompilerParams(vmem_limit_bytes=60 * 2**20),
        name="tile_sums",
    )(index, live, msg, tiles)


ORDER = ("xyz", "yzx", "zxy")


def reduce_kernel(
    part_x, part_y, part_z, self_term, out,
    q1x, q1y, q1z, pair_x, pair_y, pair_z,
    relay1x, relay1y, relay1z, got1x, got1y, got1z,
    q2x, q2y, q2z, relay2x, relay2y, relay2z, got2x, got2y, got2z,
    q3x, q3y, q3z, relay3x, relay3y, relay3z, got3x, got3y, got3z,
    send, recv, pair_send, pair_recv, local,
):
    here = place()
    parts = (part_x, part_y, part_z)
    pair = (pair_x, pair_y, pair_z)
    held = ((q1x, q1y, q1z), (q2x, q2y, q2z), (q3x, q3y, q3z))
    relay = ((relay1x, relay1y, relay1z), (relay2x, relay2y, relay2z), (relay3x, relay3y, relay3z))
    got = ((got1x, got1y, got1z), (got2x, got2y, got2z), (got3x, got3y, got3z))
    c = here["c"]
    partner = device(here, c=1)

    def owner(p, stage, step):
        return (here[ORDER[p][stage]] + step) % RING

    steps = (2, 1, 3, 0)
    pair_copies = {}
    local_copies = {}
    for n, step in enumerate(steps):
        for p in range(3):
            i = n * 3 + p
            a = owner(p, 0, step)
            local_copies[p, step] = pltpu.make_async_copy(
                parts[p].at[c, a], held[0][p].at[a], local.at[i]
            )
            pair_copies[p, step] = pltpu.make_async_remote_copy(
                src_ref=parts[p].at[1 - c, a], dst_ref=pair[p].at[a],
                send_sem=pair_send.at[i], recv_sem=pair_recv.at[i],
                device_id=partner, device_id_type=MESH,
            )
    for copy in local_copies.values():
        copy.start()
    greet([partner] + [device(here, **{axis: step}) for axis in "xyz" for step in (1, 3)])
    for copy in pair_copies.values():
        copy.start()

    def half(ref, stage, index, which):
        n = ref.shape[1] // 2
        return ref.at[index, pl.ds(which * n, n)]

    def half_of(ref, index, which):
        n = ref.shape[1] // 2
        return ref.at[index, pl.ds(which * n, n)]

    copies = {}
    count = 0
    for stage in range(3):
        for p in range(3):
            axis = ORDER[p][stage]
            source = held[stage][p]
            lead = (source.shape[1] // 2,)

            def remote(src, dst, step):
                nonlocal count
                i = count
                count += 1
                return pltpu.make_async_remote_copy(
                    src_ref=src, dst_ref=dst, send_sem=send.at[i], recv_sem=recv.at[i],
                    device_id=device(here, **{axis: step}), device_id_type=MESH,
                )

            opposite = owner(p, stage, 2)
            after, before = owner(p, stage, 1), owner(p, stage, 3)
            copies[stage, p] = dict(
                relay_a=remote(half_of(source, opposite, 0), relay[stage][p].at[0], 1),
                relay_b=remote(half_of(source, opposite, 1), relay[stage][p].at[1], 3),
                direct_after=remote(half_of(source, after, 1), half_of(got[stage][p], 0, 1), 1),
                direct_before=remote(half_of(source, before, 0), half_of(got[stage][p], 1, 0), 3),
                summed_after=remote(half_of(source, after, 0), half_of(got[stage][p], 0, 0), 1),
                summed_before=remote(half_of(source, before, 1), half_of(got[stage][p], 1, 1), 3),
            )

    def add_blocks(dst, sources, shape):
        total = 1
        for n in shape[:-2]:
            total *= n

        def one(i, carry):
            at = []
            rest = i
            for n in reversed(shape[:-2]):
                at.append(rest % n)
                rest = rest // n
            at = tuple(reversed(at))
            value = sources[0][at].astype(F32)
            for source in sources[1:]:
                value += source[at].astype(F32)
            dst[at] = value.astype(dst.dtype)
            return carry

        if total == 1:
            one(0, 0)
        else:
            lax.fori_loop(0, total, one, 0)

    for step in steps:
        for p in range(3):
            a = owner(p, 0, step)
            local_copies[p, step].wait()
            pair_copies[p, step].wait_recv()
            q = held[0][p].at[a]
            add_blocks(q, (q, pair[p].at[a]), q.shape)
            if step == 2:
                copies[0, p]["relay_a"].start()
                copies[0, p]["relay_b"].start()
            elif step == 1:
                copies[0, p]["direct_after"].start()
            elif step == 3:
                copies[0, p]["direct_before"].start()
    for stage in range(3):
        if stage > 0:
            for p in range(3):
                for name in ("relay_a", "relay_b", "direct_after", "direct_before"):
                    copies[stage, p][name].start()
        for p in range(3):
            source = held[stage][p]
            after, before = owner(p, stage, 1), owner(p, stage, 3)
            copies[stage, p]["relay_a"].wait_recv()
            mine = half_of(source, after, 0)
            add_blocks(mine, (mine, relay[stage][p].at[0]), mine.shape)
            copies[stage, p]["summed_after"].start()
            copies[stage, p]["relay_b"].wait_recv()
            mine = half_of(source, before, 1)
            add_blocks(mine, (mine, relay[stage][p].at[1]), mine.shape)
            copies[stage, p]["summed_before"].start()
        start = 0
        for p in range(3):
            for name in ("direct_after", "direct_before", "summed_after", "summed_before"):
                copies[stage, p][name].wait_recv()
            mine = held[stage][p].at[owner(p, stage, 0)]
            arrived = got[stage][p]
            if stage < 2:
                into = held[stage + 1][p]
                add_blocks(into, (mine, arrived.at[0], arrived.at[1]), into.shape)
            else:
                lanes = pl.ds(start, LANES[p])
                out[:, lanes] = (
                    mine[...].astype(F32) + arrived[0].astype(F32) + arrived[1].astype(F32)
                    + self_term[:, lanes]
                ).astype(BF)
                start += LANES[p]
    for copy in pair_copies.values():
        copy.wait_send()
    for group in copies.values():
        for copy in group.values():
            copy.wait_send()


def reduced(parts, self_term):
    def buffers(*lead):
        return [pltpu.VMEM((*lead, COLS, lanes), BF) for lanes in LANES]

    last = [pltpu.VMEM((2, COLS // 2, lanes), BF) for lanes in LANES]
    copies = 3 * 3 * 6
    return pl.pallas_call(
        reduce_kernel,
        out_shape=jax.ShapeDtypeStruct((COLS, OWN), BF),
        in_specs=[HBM, HBM, HBM, VMEM],
        out_specs=VMEM,
        scratch_shapes=[
            *buffers(RING, RING, RING),
            *buffers(RING, RING, RING),
            *buffers(2, 2, RING),
            *buffers(2, RING, RING),
            *buffers(RING, RING),
            *buffers(2, 2),
            *buffers(2, RING),
            *buffers(RING),
            *last,
            *buffers(2),
            pltpu.SemaphoreType.DMA((copies,)),
            pltpu.SemaphoreType.DMA((copies,)),
            pltpu.SemaphoreType.DMA((12,)),
            pltpu.SemaphoreType.DMA((12,)),
            pltpu.SemaphoreType.DMA((12,)),
        ],
        compiler_params=pltpu.CompilerParams(collective_id=1, has_side_effects=True),
        name="reduce_to_owner",
    )(*parts, self_term)


def body(node_feats, rel_weight, self_weight, bias, out_degree, adjacency, tile_index, tile_count):
    msg, self_term = messages(
        node_feats.T, rel_weight, self_weight, bias.reshape(1, HID), out_degree
    )
    parts = tile_sums(tile_index[0, 0].T, tile_count.reshape(1), msg, adjacency[0, 0])
    return reduced(parts, self_term).T


def solution(mesh):
    placed = (
        P("dom", "feat"),
        P(),
        P(),
        P(),
        P(None, "dom"),
        P("dom", "feat", None, None, None),
        P("dom", "feat", None, None),
        P("dom", "feat"),
    )
    return jax.shard_map(
        body, mesh=mesh, in_specs=placed, out_specs=P("dom", "feat"), check_vma=False
    )
```

time: 739 us -> 93.6 us (0.13); the launches traced: 729 us -> 93.6 us
  loops' own time: 253 us -> 0 us
  local copies, waits for them, and re-layouts: 208 us -> 2.73 us
  waiting for transfers between devices: 131 us -> 0 us
  matrix products: 107 us -> 0 us
  Pallas kernels: 0 us -> 90.2 us
  starting transfers between devices: 14.1 us -> 0 us
  between operations: 13.4 us -> 0.68 us
    another operation x1 -> x0, loops' own time: 253 us -> none  [body(): partial_value = lax.fori_loop(0, live_tiles, add_tile, partial_value)]
    dynamic_slice x257 -> x0, local copies, waits for them, and re-layouts: 130 us -> none  [the longest x128 81.8 us: add_tile(): lax.dynamic_slice_in_dim(running, target * tile_size, tile_size, 0)]
    dot_general x65 -> x0, matrix products: 107 us -> none  [the longest x64 106 us: add_tile(): jnp.dot(tile_cells.astype(jnp.bfloat16), source_msg, preferred_element_ty...]
    pallas_call x0 -> x3, Pallas kernels: none -> 90.2 us  [the longest x1 47.5 us: reduced(): pl.pallas_call(reduce_kernel, out_shape=jax.ShapeDtypeStruct((COLS, OWN),...]
    reduce_scatter x1 -> x0, waiting for transfers between devices: 86.5 us -> none  [body(): lax.psum_scatter(partial_value, 'dom', scatter_dimension=0, tiled=True)]
    dynamic_update_slice x128 -> x0, local copies, waits for them, and re-layouts: 67.4 us -> none  [add_tile(): lax.dynamic_update_slice_in_dim(running, current + contribution, target *...]
    all_to_all x2 -> x0, waiting for transfers between devices: 44.6 us -> none  [the longest x1 28.3 us: sum_at_owner(): lax.all_to_all(tiles, axis, split_axis=0, concat_axis=0, tiled=True)]
    all_to_all x2 -> x0, starting transfers between devices: 14 us -> none  [the longest x1 7.15 us: copy_for_each(): return lax.all_to_all(copies, axis, split_axis=0, concat_axis=0, tiled=True)]
  transfers between devices with their start and end apart: 3 -> 0, of which waited for: 3 -> 0; matrix products, arithmetic and copies ran while one was open for 0% -> 0% of each run, Pallas kernels for 0% -> 0%
where the time goes in v1:
time: 93.6 us
  Pallas kernels  90.2 us (96%)
  local copies, waits for them, and re-layouts  2.73 us (3%)
    pallas_call x1, Pallas kernels, reduced(): pl.pallas_call(reduce_kernel, out_shape=jax.ShapeDtypeStruct((COLS, OWN),...  47.5 us
    pallas_call x1, Pallas kernels, messages(): pl.pallas_call(messages_kernel, out_shape=(jax.ShapeDtypeStruct((REL * 4,...  24.9 us
    pallas_call x1, Pallas kernels, tile_sums(): pl.pallas_call(tiles_kernel, out_shape=tuple((jax.ShapeDtypeStruct((2, RI...  17.8 us
    unnamed x2, local copies, waits for them, and re-layouts  2.73 us

profile of v1, /device:TPU:0, one launch (start us, length us, event | category | flops | bytes accessed | tf_op | source)
XLA Modules:
  0.0 93.6 jit_solution(4043936574937885039)
XLA Ops:
  0.7 1.3 %copy.11 = s32[1,1,64,3]{2,3,1,0:T(4,128)} copy(s32[1,1,64,3]{2,1,3,0:T(1,128)} %param.14) | data formatting | bytes 1536
  1.9 24.9 %messages.1 = (bf16[16,512,256]{2,1,0:T(8,128)(2,1)}, f32[32,1024]{1,0:T(8,128)}) custom-call(bf16[32,1024]{1,0:T(8,128)(2,1)} %bitcast.13, bf16[4,512,512]{2,1,0:T(8,128)(2,1)} %rel.1, bf16[512,512]{1,0:T(8,128)(2,1)} %own.1, f32[1,512]{1,0:T(1,128)} %bitcast.15, s32[4,1024]{1,0:T(4,128)} %degree.1), custom_call_target="tpu_custom_call" | custom-call | tf_op jit(solution)/shard_map/messages/pallas_call | solution.py:184
  26.8 17.8 %tile_sums.1 = (bf16[2,4,4,4,32,384]{5,4,3,2,1,0:T(8,128)(2,1)}, bf16[2,4,4,4,32,384]{5,4,3,2,1,0:T(8,128)(2,1)}, bf16[2,4,4,4,32,256]{5,4,3,2,1,0:T(8,128)(2,1)}) custom-call(s32[3,64]{1,0:T(4,128)} %bitcast.14, s32[1]{0:T(128)} %bitcast.10.live, bf16[16,512,256]{2,1,0:T(8,128)(2,1)} %get-tuple-element.10.msg, s32[64,256,256]{2,1,0:T(8,128)} %bitcast.11), custom_call_target="tpu_custom_call" | custom-call | tf_op jit(solution)/shard_map/tile_sums/pallas_call | solution.py:257
  44.6 47.5 %reduce_to_owner.1 = bf16[32,1024]{1,0:T(8,128)(2,1)} custom-call(bf16[2,4,4,4,32,384]{5,4,3,2,1,0:T(8,128)(2,1)} %get-tuple-element.11.part_x, bf16[2,4,4,4,32,384]{5,4,3,2,1,0:T(8,128)(2,1)} %get-tuple-element.12.part_y, bf16[2,4,4,4,32,256]{5,4,3,2,1,0:T(8,128)(2,1)} %get-tuple-element.13.part_z, f32[32,1024]{1,0:T(8,128)} %get-tuple-element.14.self_term), custom_call_target="tpu_custom_call" | custom-call | tf_op jit(solution)/shard_map/reduce_to_owner/pallas_call | solution.py:436
  92.1 1.5 %copy.14 = bf16[1024,32]{0,1:T(8,128)(2,1)} copy(bf16[1024,32]{0,1:T(8,128)(2,1)} %bitcast.12) | data formatting | bytes 131072

commit v2 on v0

v2 whole, which is shorter than its diff:
```python
import jax
import jax.numpy as jnp
from jax import lax
from jax.experimental import pallas as pl
from jax.experimental.pallas import tpu as pltpu
from jax.sharding import PartitionSpec as P

MESH = pl.DeviceIdType.MESH
BF = jnp.bfloat16
F32 = jnp.float32
I32 = jnp.int32
RING = 4
HID = 512
COLS = 32
ROWS = 16
OWN = 1024
TILE = 256
SLOTS = 64
REL = 4
BLOCKS = 32
HALVES = 2
BATCH = 4
DEPTH = 4
UNROLL = 8
LANES = (384, 384, 256)
ORDER = ("xyz", "yzx", "zxy")
STEPS = (2, 1, 3, 0)
VMEM = pl.BlockSpec(memory_space=pltpu.VMEM)
SMEM = pl.BlockSpec(memory_space=pltpu.SMEM)
HBM = pl.BlockSpec(memory_space=pl.ANY)
NT = (((1,), (1,)), ((), ()))
GATHER_COPIES = 2 * (3 + 8 + 8)
RING_COPIES = HALVES * 3 * 3 * 6
PAIR_COPIES = HALVES * 12


def place():
    dom = lax.axis_index("dom")
    feat = lax.axis_index("feat")
    return dict(z=dom // 2, c=dom % 2, x=feat // RING, y=feat % RING)


def device(here, **moved):
    at = dict(here)
    for axis, step in moved.items():
        at[axis] = (at[axis] + step) % (2 if axis == "c" else RING)
    return (at["z"] * 2 + at["c"], at["x"] * RING + at["y"])


def greet(peers):
    barrier = pltpu.get_barrier_semaphore()
    for peer in peers:
        pl.semaphore_signal(barrier, inc=1, device_id=peer, device_id_type=MESH)
    pl.semaphore_wait(barrier, len(peers))


def aligned(start, size):
    return pl.ds(pl.multiple_of(start, size), size)


def sort_slots(index, live, table):
    shape = (128, 128)
    across = lax.broadcasted_iota(I32, shape, 1)
    down = lax.broadcasted_iota(I32, shape, 0)

    def row(value):
        return jnp.broadcast_to(jnp.concatenate([value, value], axis=1), shape)

    is_live = across < live
    target = jnp.where(is_live, row(index[1]), BLOCKS)
    block = row(index[0]) * 4 + row(index[2])
    key = jnp.where(across < SLOTS, target * 128 + across, 65536 + across)
    key_down = key.T
    rank = jnp.sum(jnp.where(key_down < key, 1, 0), axis=0, keepdims=True)
    rank_down = jnp.broadcast_to(rank, shape).T
    hit = rank_down == across
    target_down = target.T
    table[0:1, :] = jnp.sum(jnp.where(hit, down, 0), axis=0, keepdims=True)
    table[1:2, :] = jnp.sum(jnp.where(hit, block.T, 0), axis=0, keepdims=True)
    table[2:3, :] = jnp.sum(jnp.where(hit, target_down, 0), axis=0, keepdims=True)
    real = down < SLOTS
    upto = jnp.sum(jnp.where(real & (target_down <= across), 1, 0), axis=0, keepdims=True)
    below = jnp.sum(jnp.where(real & (target_down < across), 1, 0), axis=0, keepdims=True)
    table[3:4, :] = jnp.where(upto > below, upto, 0)


def kernel(
    nodes, rel, own, bias, degree, index, live, tiles, out,
    feats, rel_in, own_in, rel_t, own_t, bias_t, self_term, inverse, msg,
    raw, cells, sums, table, order,
    out_x, out_y, out_z, pair_x, pair_y, pair_z,
    q1x, q1y, q1z, relay1x, relay1y, relay1z, got1x, got1y, got1z,
    q2x, q2y, q2z, relay2x, relay2y, relay2z, got2x, got2y, got2z,
    q3x, q3y, q3z, relay3x, relay3y, relay3z, got3x, got3y, got3z,
    gather_send, gather_recv, pair_send, pair_recv, ring_send, ring_recv, local, arrived,
):
    here = place()
    outgoing = (out_x, out_y, out_z)
    pair = (pair_x, pair_y, pair_z)
    held = ((q1x, q1y, q1z), (q2x, q2y, q2z), (q3x, q3y, q3z))
    relays = ((relay1x, relay1y, relay1z), (relay2x, relay2y, relay2z), (relay3x, relay3y, relay3z))
    gots = ((got1x, got1y, got1z), (got2x, got2y, got2z), (got3x, got3y, got3z))
    c = here["c"]

    fetch_rel = pltpu.make_async_copy(rel, rel_in, local.at[0])
    fetch_own = pltpu.make_async_copy(own, own_in, local.at[1])
    fetch_rel.start()
    fetch_own.start()

    def fetch_tiles(batch, slot):
        return pltpu.make_async_copy(
            tiles.at[pl.ds(batch * BATCH, BATCH)], raw.at[slot], arrived.at[slot]
        )

    for batch in range(DEPTH):
        fetch_tiles(batch, batch).start()
    partner = device(here, c=1)
    peers = [device(here, **{axis: step}) for axis in "xy" for step in (1, 2, 3)]
    peers += [device(here, z=step) for step in (1, 3)] + [partner]
    greet(peers)

    half = COLS // 2
    first_axis = ("x", "y")
    second_axis = ("y", "x")

    def rows(h, x, y):
        return aligned((x * RING + y) * COLS + h * half, half)

    counts = dict(gather=0, ring=0)

    def remote(src, dst, peer):
        i = counts["gather"]
        counts["gather"] += 1
        return pltpu.make_async_remote_copy(
            src_ref=src, dst_ref=dst, send_sem=gather_send.at[i], recv_sem=gather_recv.at[i],
            device_id=peer, device_id_type=MESH,
        )

    def part(h, a, b, lanes=pl.ds(0, OWN)):
        moved = {first_axis[h]: a, second_axis[h]: b}
        at = rows(h, (here["x"] + moved["x"]) % RING, (here["y"] + moved["y"]) % RING)
        return feats.at[at, lanes]

    for h in (0, 1):
        feats[rows(h, here["x"], here["y"]), :] = nodes[pl.ds(h * half, half), :]
    first, second, relay = {}, {}, {}
    left, right = pl.ds(0, OWN // 2), pl.ds(OWN // 2, OWN // 2)
    for h in (0, 1):
        src = nodes.at[pl.ds(h * half, half), :]
        for step in (1, 3, 2):
            first[h, step] = remote(src, part(h, 0, 0), device(here, **{first_axis[h]: step}))
        for a in (0, 1, 3, 2):
            for step in (1, 3):
                second[h, a, step] = remote(
                    src if a == 0 else part(h, a, 0), part(h, a, 0),
                    device(here, **{second_axis[h]: step}),
                )
            relay[h, a, 1] = remote(
                part(h, a, 3, left), part(h, a, 3, left), device(here, **{second_axis[h]: 1})
            )
            relay[h, a, 3] = remote(
                part(h, a, 1, right), part(h, a, 1, right), device(here, **{second_axis[h]: 3})
            )
    for step in (1, 3, 2):
        for h in (0, 1):
            first[h, step].start()
    for step in (1, 3):
        for h in (0, 1):
            second[h, 0, step].start()

    def transpose(r):
        turned = rel_in[r].T.reshape(HID // COLS, HALVES, ROWS, HID)
        for h in range(HALVES):
            rel_t[r, h] = turned[:, h].reshape(HID // 2, HID)

    def convert(low, high):
        def one(batch, carry):
            slot = batch % DEPTH
            fetch_tiles(batch, slot).wait()

            def tile(i, carry):
                cells[batch * BATCH + i] = raw[slot, i].astype(F32).astype(BF)
                return carry

            lax.fori_loop(0, BATCH, tile, 0, unroll=2)

            @pl.when(batch + DEPTH < SLOTS // BATCH)
            def _():
                fetch_tiles(batch + DEPTH, slot).start()

            return carry

        lax.fori_loop(low, high, one, 0)

    inverse[...] = 1.0 / jnp.maximum(degree[...], 1).astype(F32)
    sort_slots(index, live[0, 0], table)
    fetch_order = pltpu.make_async_copy(table, order, local.at[2])
    fetch_order.start()
    sums[0] = jnp.zeros((HID // 2, TILE), F32)
    fetch_rel.wait()
    fetch_own.wait()
    transpose(0)
    transpose(1)
    convert(0, 2)
    for a in (3, 1):
        for h in (0, 1):
            first[h, RING - a].wait_recv()
            second[h, a, 1].start()
            second[h, a, 3].start()
    transpose(2)
    for h in (0, 1):
        second[h, 0, 1].wait_recv()
        relay[h, 0, 1].start()
        second[h, 0, 3].wait_recv()
        relay[h, 0, 3].start()
    for h in (0, 1):
        first[h, 2].wait_recv()
        second[h, 2, 1].start()
        second[h, 2, 3].start()
    transpose(3)
    convert(2, 6)
    for a in (3, 1):
        for h in (0, 1):
            second[h, a, 1].wait_recv()
            relay[h, a, 1].start()
            second[h, a, 3].wait_recv()
            relay[h, a, 3].start()
    convert(6, 10)
    for h in (0, 1):
        second[h, 2, 1].wait_recv()
        relay[h, 2, 1].start()
        second[h, 2, 3].wait_recv()
        relay[h, 2, 3].start()
    own_t[...] = own_in[...].T
    bias_t[...] = jnp.broadcast_to(bias[...], (128, HID)).T
    convert(10, 16)
    fetch_order.wait()
    for a in (0, 3, 1, 2):
        for h in (0, 1):
            relay[h, a, 1].wait_recv()
            relay[h, a, 3].wait_recv()

    def make_messages(h):
        for s in range(OWN // TILE):
            at = pl.ds(s * TILE, TILE)

            def relation(r, carry):
                product = jnp.dot(rel_t[r, h], feats[:, at], preferred_element_type=F32)
                msg[h, r * 4 + s] = (product * inverse[pl.ds(r, 1), at]).astype(BF)
                return carry

            lax.fori_loop(0, REL, relation, 0, unroll=True)

    def make_self_term():
        mine = aligned((here["x"] * RING + here["y"]) * COLS, COLS)
        bias_rows = bias_t[mine, :]
        for s in range(OWN // TILE):
            at = pl.ds(s * TILE, TILE)
            self_term[:, at] = jnp.dot(
                own_t[mine, :], feats[:, at], preferred_element_type=F32
            ) + jnp.concatenate([bias_rows, bias_rows], axis=1)

    def add_tiles(h, low, high):
        def some(i, carry):
            for u in range(UNROLL):
                t = i * UNROLL + u
                product = lax.dot_general(
                    msg[h, order[1, t]], cells[order[0, t]], NT, preferred_element_type=F32
                )
                before = order[2, jnp.maximum(t - 1, 0)]
                same = jnp.where((t > 0) & (order[2, t] == before), 1.0, 0.0)
                sums[t + 1] = sums[t] * same + product
            return carry

        lax.fori_loop(low // UNROLL, high // UNROLL, some, 0)

    def owner(p, stage, step):
        return (here[ORDER[p][stage]] + step) % RING

    def build(p, h, a, core, dst):
        def one(i, carry):
            m, n = i // RING, i % RING
            if p == 0:
                x, y, z = a, m, n
            elif p == 1:
                x, y, z = n, a, m
            else:
                x, y, z = m, n, a
            at = aligned((x * RING + y) * ROWS, ROWS)
            base = z * 8 + core * 4
            if p == 0:
                dst[m, n, :, 0:256] = sums[order[3, base], at, :].astype(BF)
                dst[m, n, :, 256:384] = sums[order[3, base + 1], at, 0:128].astype(BF)
            elif p == 1:
                dst[m, n, :, 0:128] = sums[order[3, base + 1], at, 128:256].astype(BF)
                dst[m, n, :, 128:384] = sums[order[3, base + 2], at, :].astype(BF)
            else:
                dst[m, n] = sums[order[3, base + 3], at, :].astype(BF)
            return carry

        lax.fori_loop(0, RING * RING, one, 0, unroll=4)

    pair_copies = {}
    for h in range(HALVES):
        for n, step in enumerate(STEPS):
            for p in range(3):
                i = (h * 4 + n) * 3 + p
                a = owner(p, 0, step)
                pair_copies[h, p, step] = pltpu.make_async_remote_copy(
                    src_ref=outgoing[p].at[h, a], dst_ref=pair[p].at[h, a],
                    send_sem=pair_send.at[i], recv_sem=pair_recv.at[i],
                    device_id=partner, device_id_type=MESH,
                )

    def half_of(ref, lead, which):
        n = ref.shape[len(lead)] // 2
        return ref.at[(*lead, pl.ds(which * n, n))]

    ring = {}
    for h in range(HALVES):
        for stage in range(3):
            for p in range(3):
                axis = ORDER[p][stage]
                source, via, got = held[stage][p], relays[stage][p], gots[stage][p]

                def step_copy(src, dst, step):
                    i = counts["ring"]
                    counts["ring"] += 1
                    return pltpu.make_async_remote_copy(
                        src_ref=src, dst_ref=dst, send_sem=ring_send.at[i],
                        recv_sem=ring_recv.at[i],
                        device_id=device(here, **{axis: step}), device_id_type=MESH,
                    )

                opposite = owner(p, stage, 2)
                after, before = owner(p, stage, 1), owner(p, stage, 3)
                ring[h, stage, p] = dict(
                    relay_a=step_copy(half_of(source, (h, opposite), 0), via.at[h, 0], 1),
                    relay_b=step_copy(half_of(source, (h, opposite), 1), via.at[h, 1], 3),
                    direct_after=step_copy(
                        half_of(source, (h, after), 1), half_of(got, (h, 0), 1), 1
                    ),
                    direct_before=step_copy(
                        half_of(source, (h, before), 0), half_of(got, (h, 1), 0), 3
                    ),
                    summed_after=step_copy(
                        half_of(source, (h, after), 0), half_of(got, (h, 0), 0), 1
                    ),
                    summed_before=step_copy(
                        half_of(source, (h, before), 1), half_of(got, (h, 1), 1), 3
                    ),
                )

    def add_blocks(dst, sources):
        lead = dst.shape[:-3]
        total = 1
        for n in lead:
            total *= n

        def one(i, carry):
            at = []
            rest = i
            for n in reversed(lead):
                at.append(rest % n)
                rest = rest // n
            at = tuple(reversed(at))
            value = sources[0][at].astype(F32)
            for source in sources[1:]:
                value += source[at].astype(F32)
            dst[at] = value.astype(dst.dtype)
            return carry

        if total == 1:
            one(0, 0)
        else:
            lax.fori_loop(0, total, one, 0)

    def send_to_partner(h):
        for step in STEPS:
            for p in range(3):
                a = owner(p, 0, step)
                build(p, h, a, 1 - c, outgoing[p].at[h, a])
                pair_copies[h, p, step].start()

    def build_own(h):
        for step in STEPS:
            for p in range(3):
                a = owner(p, 0, step)
                build(p, h, a, c, held[0][p].at[h, a])

    def join_partner(h, step):
        for p in range(3):
            a = owner(p, 0, step)
            pair_copies[h, p, step].wait_recv()
            q = held[0][p].at[h, a]
            add_blocks(q, (q, pair[p].at[h, a]))
            if step == 2:
                ring[h, 0, p]["relay_a"].start()
                ring[h, 0, p]["relay_b"].start()
            elif step == 1:
                ring[h, 0, p]["direct_after"].start()
            elif step == 3:
                ring[h, 0, p]["direct_before"].start()

    def start_stage(h, stage):
        for p in range(3):
            for name in ("relay_a", "relay_b"):
                ring[h, stage, p][name].start()
        for p in range(3):
            for name in ("direct_after", "direct_before"):
                ring[h, stage, p][name].start()

    def pass_on(h, stage):
        for p in range(3):
            source, via, copies = held[stage][p], relays[stage][p], ring[h, stage, p]
            copies["relay_a"].wait_recv()
            mine = half_of(source, (h, owner(p, stage, 1)), 0)
            add_blocks(mine, (mine, via.at[h, 0])) if stage < 2 else add_flat(mine, via.at[h, 0])
            copies["summed_after"].start()
            copies["relay_b"].wait_recv()
            mine = half_of(source, (h, owner(p, stage, 3)), 1)
            add_blocks(mine, (mine, via.at[h, 1])) if stage < 2 else add_flat(mine, via.at[h, 1])
            copies["summed_before"].start()

    def add_flat(dst, other):
        dst[...] = dst[...] + other[...]

    def finish_stage(h, stage):
        start = 0
        for p in range(3):
            for name in ("direct_after", "direct_before", "summed_after", "summed_before"):
                ring[h, stage, p][name].wait_recv()
            mine = held[stage][p].at[h, owner(p, stage, 0)]
            got = gots[stage][p]
            if stage < 2:
                add_blocks(held[stage + 1][p].at[h], (mine, got.at[h, 0], got.at[h, 1]))
            else:
                at = pl.ds(h * ROWS, ROWS)
                lanes = pl.ds(start, LANES[p])
                out[at, lanes] = (
                    mine[...] + got[h, 0] + got[h, 1] + self_term[at, lanes]
                ).astype(BF)
                start += LANES[p]

    make_messages(0)
    add_tiles(0, 0, SLOTS)
    send_to_partner(0)
    build_own(0)
    join_partner(0, 2)
    make_messages(1)
    for step in (1, 3, 0):
        join_partner(0, step)
    add_tiles(1, 0, 40)
    pass_on(0, 0)
    add_tiles(1, 40, SLOTS)
    send_to_partner(1)
    build_own(1)
    join_partner(1, 2)
    finish_stage(0, 0)
    start_stage(0, 1)
    for step in (1, 3, 0):
        join_partner(1, step)
    make_self_term()
    pass_on(0, 1)
    pass_on(1, 0)
    finish_stage(0, 1)
    start_stage(0, 2)
    finish_stage(1, 0)
    start_stage(1, 1)
    pass_on(0, 2)
    pass_on(1, 1)
    finish_stage(0, 2)
    finish_stage(1, 1)
    start_stage(1, 2)
    pass_on(1, 2)
    finish_stage(1, 2)
    for copies in (first, second, relay, pair_copies):
        for copy in copies.values():
            copy.wait_send()
    for copies in ring.values():
        for copy in copies.values():
            copy.wait_send()


def body(node_feats, rel_weight, self_weight, bias, out_degree, adjacency, tile_index, tile_count):
    def buffers(*lead, kind=BF, rows=ROWS):
        return [pltpu.VMEM((HALVES, *lead, rows, lanes), kind) for lanes in LANES]

    result = pl.pallas_call(
        kernel,
        out_shape=jax.ShapeDtypeStruct((COLS, OWN), BF),
        in_specs=[VMEM, HBM, HBM, VMEM, VMEM, VMEM, SMEM, HBM],
        out_specs=VMEM,
        scratch_shapes=[
            pltpu.VMEM((HID, OWN), BF),
            pltpu.VMEM((REL, HID, HID), BF),
            pltpu.VMEM((HID, HID), BF),
            pltpu.VMEM((REL, HALVES, HID // 2, HID), BF),
            pltpu.VMEM((HID, HID), BF),
            pltpu.VMEM((HID, 128), F32),
            pltpu.VMEM((COLS, OWN), F32),
            pltpu.VMEM((REL, OWN), F32),
            pltpu.VMEM((HALVES, REL * 4, HID // 2, TILE), BF),
            pltpu.VMEM((DEPTH, BATCH, TILE, TILE), I32),
            pltpu.VMEM((SLOTS, TILE, TILE), BF),
            pltpu.VMEM((SLOTS + 1, HID // 2, TILE), F32),
            pltpu.VMEM((8, 128), I32),
            pltpu.SMEM((8, 128), I32),
            *buffers(RING, RING, RING),
            *buffers(RING, RING, RING),
            *buffers(RING, RING, RING),
            *buffers(2, 2, RING),
            *buffers(2, RING, RING),
            *buffers(RING, RING),
            *buffers(2, 2),
            *buffers(2, RING),
            *buffers(RING, kind=F32),
            *buffers(2, kind=F32, rows=ROWS // 2),
            *buffers(2, kind=F32),
            pltpu.SemaphoreType.DMA((GATHER_COPIES,)),
            pltpu.SemaphoreType.DMA((GATHER_COPIES,)),
            pltpu.SemaphoreType.DMA((PAIR_COPIES,)),
            pltpu.SemaphoreType.DMA((PAIR_COPIES,)),
            pltpu.SemaphoreType.DMA((RING_COPIES,)),
            pltpu.SemaphoreType.DMA((RING_COPIES,)),
            pltpu.SemaphoreType.DMA((3,)),
            pltpu.SemaphoreType.DMA((DEPTH,)),
        ],
        compiler_params=pltpu.CompilerParams(
            collective_id=0, has_side_effects=True, vmem_limit_bytes=63 * 2**20
        ),
        name="relational_layer",
    )(
        node_feats.T, rel_weight, self_weight, bias.reshape(1, HID), out_degree,
        jnp.transpose(tile_index[0], (2, 0, 1)), tile_count, adjacency[0, 0],
    )
    return result.T


def solution(mesh):
    placed = (
        P("dom", "feat"),
        P(),
        P(),
        P(),
        P(None, "dom"),
        P("dom", "feat", None, None, None),
        P("dom", "feat", None, None),
        P("dom", "feat"),
    )
    return jax.shard_map(
        body, mesh=mesh, in_specs=placed, out_specs=P("dom", "feat"), check_vma=False
    )
```

time: 739 us -> 72.4 us (0.10); the launches traced: 729 us -> 72.2 us
  loops' own time: 253 us -> 0 us
  local copies, waits for them, and re-layouts: 208 us -> 1.47 us
  waiting for transfers between devices: 131 us -> 0 us
  matrix products: 107 us -> 0 us
  Pallas kernels: 0 us -> 70 us
  starting transfers between devices: 14.1 us -> 0 us
  between operations: 13.4 us -> 0.66 us
    another operation x1 -> x0, loops' own time: 253 us -> none  [body(): partial_value = lax.fori_loop(0, live_tiles, add_tile, partial_value)]
    dynamic_slice x257 -> x0, local copies, waits for them, and re-layouts: 130 us -> none  [the longest x128 81.8 us: add_tile(): lax.dynamic_slice_in_dim(running, target * tile_size, tile_size, 0)]
    dot_general x65 -> x0, matrix products: 107 us -> none  [the longest x64 106 us: add_tile(): jnp.dot(tile_cells.astype(jnp.bfloat16), source_msg, preferred_element_ty...]
    reduce_scatter x1 -> x0, waiting for transfers between devices: 86.5 us -> none  [body(): lax.psum_scatter(partial_value, 'dom', scatter_dimension=0, tiled=True)]
    pallas_call x0 -> x1, Pallas kernels: none -> 70 us  [body(): pl.pallas_call(kernel, out_shape=jax.ShapeDtypeStruct((COLS, OWN), BF), i...]
    dynamic_update_slice x128 -> x0, local copies, waits for them, and re-layouts: 67.4 us -> none  [add_tile(): lax.dynamic_update_slice_in_dim(running, current + contribution, target *...]
    all_to_all x2 -> x0, waiting for transfers between devices: 44.6 us -> none  [the longest x1 28.3 us: sum_at_owner(): lax.all_to_all(tiles, axis, split_axis=0, concat_axis=0, tiled=True)]
    all_to_all x2 -> x0, starting transfers between devices: 14 us -> none  [the longest x1 7.15 us: copy_for_each(): return lax.all_to_all(copies, axis, split_axis=0, concat_axis=0, tiled=True)]
  transfers between devices with their start and end apart: 3 -> 0, of which waited for: 3 -> 0; matrix products, arithmetic and copies ran while one was open for 0% -> 0% of each run, Pallas kernels for 0% -> 0%
where the time goes in v2:
time: 72.4 us; the launch traced here: 72.2 us
  Pallas kernels  70 us (97%)
  local copies, waits for them, and re-layouts  1.47 us (2%)
    pallas_call x1, Pallas kernels, body(): pl.pallas_call(kernel, out_shape=jax.ShapeDtypeStruct((COLS, OWN), BF), i...  70 us
    unnamed x1, local copies, waits for them, and re-layouts  1.47 us

profile of v2, /device:TPU:0, one launch (start us, length us, event | category | flops | bytes accessed | tf_op | source)
XLA Modules:
  0.0 72.2 jit_solution(11908147018902028709)
XLA Ops:
  0.7 70.0 %relational_layer.1 = bf16[32,1024]{1,0:T(8,128)(2,1)} custom-call(bf16[32,1024]{1,0:T(8,128)(2,1)} %bitcast.9, bf16[4,512,512]{2,1,0:T(8,128)(2,1)} %rel.1, bf16[512,512]{1,0:T(8,128)(2,1)} %own.1, f32[1,512]{1,0:T(1,128)} %bitcast.10, s32[4,1024]{1,0:T(4,128)} %degree.1, s32[3,1,64]{2,1,0:T(1,128)} %bitcast.11, s32[1,1]{1,0:T(1,128)S(6)} %copy.10.live, ...), custom_call_target="tpu_custom_call" | custom-call | tf_op jit(solution)/shard_map/relational_layer/pallas_call | solution.py:489
  70.7 1.5 %copy.11 = bf16[1024,32]{0,1:T(8,128)(2,1)} copy(bf16[1024,32]{0,1:T(8,128)(2,1)} %bitcast.8) | data formatting | bytes 131072

commit v3 on v2

--- a/solution.py
+++ b/solution.py
@@ -25,13 +25,14 @@
 LANES = (384, 384, 256)
 ORDER = ("xyz", "yzx", "zxy")
 STEPS = (2, 1, 3, 0)
+DIRECT = (False, True, True)
 VMEM = pl.BlockSpec(memory_space=pltpu.VMEM)
 SMEM = pl.BlockSpec(memory_space=pltpu.SMEM)
 HBM = pl.BlockSpec(memory_space=pl.ANY)
 NT = (((1,), (1,)), ((), ()))
-GATHER_COPIES = 2 * (3 + 8 + 8)
-RING_COPIES = HALVES * 3 * 3 * 6
-PAIR_COPIES = HALVES * 12
+GATHER_ARRIVALS = 2 * (3 + 8) + 1
+PAIR_ARRIVALS = HALVES * 12
+RING_ARRIVALS = HALVES * 3 * sum(1 if direct else 3 for direct in DIRECT)
 
 
 def place():
@@ -85,14 +86,14 @@
 
 
 def kernel(
-    nodes, rel, own, bias, degree, index, live, tiles, out,
-    feats, rel_in, own_in, rel_t, own_t, bias_t, self_term, inverse, msg,
+    nodes, rel, own, bias, degree, index, live, tiles, result,
+    out,    feats, rel_in, own_in, rel_t, own_t, bias_t, self_term, inverse, msg,
     raw, cells, sums, table, order,
     out_x, out_y, out_z, pair_x, pair_y, pair_z,
     q1x, q1y, q1z, relay1x, relay1y, relay1z, got1x, got1y, got1z,
     q2x, q2y, q2z, relay2x, relay2y, relay2z, got2x, got2y, got2z,
     q3x, q3y, q3z, relay3x, relay3y, relay3z, got3x, got3y, got3z,
-    gather_send, gather_recv, pair_send, pair_recv, ring_send, ring_recv, local, arrived,
+    sent, gather_recv, pair_recv, ring_recv, local, arrived,
 ):
     here = place()
     outgoing = (out_x, out_y, out_z)
@@ -128,11 +129,12 @@
 
     counts = dict(gather=0, ring=0)
 
-    def remote(src, dst, peer):
-        i = counts["gather"]
-        counts["gather"] += 1
+    def remote(src, dst, peer, arrival=None):
+        if arrival is None:
+            arrival = counts["gather"]
+            counts["gather"] += 1
         return pltpu.make_async_remote_copy(
-            src_ref=src, dst_ref=dst, send_sem=gather_send.at[i], recv_sem=gather_recv.at[i],
+            src_ref=src, dst_ref=dst, send_sem=sent.at[0], recv_sem=gather_recv.at[arrival],
             device_id=peer, device_id_type=MESH,
         )
 
@@ -156,10 +158,12 @@
                     device(here, **{second_axis[h]: step}),
                 )
             relay[h, a, 1] = remote(
-                part(h, a, 3, left), part(h, a, 3, left), device(here, **{second_axis[h]: 1})
+                part(h, a, 3, left), part(h, a, 3, left), device(here, **{second_axis[h]: 1}),
+                GATHER_ARRIVALS - 1,
             )
             relay[h, a, 3] = remote(
-                part(h, a, 1, right), part(h, a, 1, right), device(here, **{second_axis[h]: 3})
+                part(h, a, 1, right), part(h, a, 1, right), device(here, **{second_axis[h]: 3}),
+                GATHER_ARRIVALS - 1,
             )
     for step in (1, 3, 2):
         for h in (0, 1):
@@ -235,10 +239,9 @@
     bias_t[...] = jnp.broadcast_to(bias[...], (128, HID)).T
     convert(10, 16)
     fetch_order.wait()
-    for a in (0, 3, 1, 2):
-        for h in (0, 1):
-            relay[h, a, 1].wait_recv()
-            relay[h, a, 3].wait_recv()
+    pltpu.make_async_copy(
+        feats.at[pl.ds(0, 128)], feats.at[pl.ds(0, 128)], gather_recv.at[GATHER_ARRIVALS - 1]
+    ).wait()
 
     def make_messages(h):
         for s in range(OWN // TILE):
@@ -277,28 +280,43 @@
     def owner(p, stage, step):
         return (here[ORDER[p][stage]] + step) % RING
 
-    def build(p, h, a, core, dst):
+    def own_blocks(p, a, core, i):
+        if p == 0:
+            at = aligned(a * RING * ROWS, RING * ROWS)
+            base = i * 8 + core * 4
+            shape = (RING, ROWS, -1)
+            yield (slice(None), i, slice(None), pl.ds(0, 256)), sums[order[3, base], at, :].reshape(
+                RING, ROWS, 256
+            )
+            yield (slice(None), i, slice(None), pl.ds(256, 128)), sums[
+                order[3, base + 1], at, 0:128
+            ].reshape(RING, ROWS, 128)
+        elif p == 1:
+            base = i * 8 + core * 4
+            for x in range(RING):
+                at = aligned((x * RING + a) * ROWS, ROWS)
+                yield (i, x, slice(None), pl.ds(0, 128)), sums[order[3, base + 1], at, 128:256]
+                yield (i, x, slice(None), pl.ds(128, 256)), sums[order[3, base + 2], at, :]
+        else:
+            at = aligned(i * RING * ROWS, RING * ROWS)
+            base = a * 8 + core * 4
+            yield (i,), sums[order[3, base + 3], at, :].reshape(RING, ROWS, 256)
+
+    def build(p, a, core, dst):
         def one(i, carry):
-            m, n = i // RING, i % RING
-            if p == 0:
-                x, y, z = a, m, n
-            elif p == 1:
-                x, y, z = n, a, m
-            else:
-                x, y, z = m, n, a
-            at = aligned((x * RING + y) * ROWS, ROWS)
-            base = z * 8 + core * 4
-            if p == 0:
-                dst[m, n, :, 0:256] = sums[order[3, base], at, :].astype(BF)
-                dst[m, n, :, 256:384] = sums[order[3, base + 1], at, 0:128].astype(BF)
-            elif p == 1:
-                dst[m, n, :, 0:128] = sums[order[3, base + 1], at, 128:256].astype(BF)
-                dst[m, n, :, 128:384] = sums[order[3, base + 2], at, :].astype(BF)
-            else:
-                dst[m, n] = sums[order[3, base + 3], at, :].astype(BF)
+            for at, value in own_blocks(p, a, core, i):
+                dst[at] = value.astype(BF)
             return carry
 
-        lax.fori_loop(0, RING * RING, one, 0, unroll=4)
+        lax.fori_loop(0, RING, one, 0, unroll=True)
+
+    def build_joined(p, a, core, dst, other):
+        def one(i, carry):
+            for at, value in own_blocks(p, a, core, i):
+                dst[at] = (value + other[at].astype(F32)).astype(BF)
+            return carry
+
+        lax.fori_loop(0, RING, one, 0, unroll=True)
 
     pair_copies = {}
     for h in range(HALVES):
@@ -308,7 +326,7 @@
                 a = owner(p, 0, step)
                 pair_copies[h, p, step] = pltpu.make_async_remote_copy(
                     src_ref=outgoing[p].at[h, a], dst_ref=pair[p].at[h, a],
-                    send_sem=pair_send.at[i], recv_sem=pair_recv.at[i],
+                    send_sem=sent.at[1 + p], recv_sem=pair_recv.at[i],
                     device_id=partner, device_id_type=MESH,
                 )
 
@@ -323,20 +341,34 @@
                 axis = ORDER[p][stage]
                 source, via, got = held[stage][p], relays[stage][p], gots[stage][p]
 
-                def step_copy(src, dst, step):
-                    i = counts["ring"]
-                    counts["ring"] += 1
+                joint = counts["ring"]
+                counts["ring"] += 1
+
+                def step_copy(src, dst, step, alone=False):
+                    arrival = joint
+                    if alone:
+                        arrival = counts["ring"]
+                        counts["ring"] += 1
                     return pltpu.make_async_remote_copy(
-                        src_ref=src, dst_ref=dst, send_sem=ring_send.at[i],
-                        recv_sem=ring_recv.at[i],
+                        src_ref=src, dst_ref=dst, send_sem=sent.at[4 + stage * 3 + p],
+                        recv_sem=ring_recv.at[arrival],
                         device_id=device(here, **{axis: step}), device_id_type=MESH,
                     )
 
                 opposite = owner(p, stage, 2)
                 after, before = owner(p, stage, 1), owner(p, stage, 3)
+                if DIRECT[stage]:
+                    ring[h, stage, p] = dict(
+                        joint=joint,
+                        opposite=step_copy(source.at[h, opposite], got.at[h, 2], 2),
+                        after=step_copy(source.at[h, after], got.at[h, 0], 1),
+                        before=step_copy(source.at[h, before], got.at[h, 1], 3),
+                    )
+                    continue
                 ring[h, stage, p] = dict(
-                    relay_a=step_copy(half_of(source, (h, opposite), 0), via.at[h, 0], 1),
-                    relay_b=step_copy(half_of(source, (h, opposite), 1), via.at[h, 1], 3),
+                    joint=joint,
+                    relay_a=step_copy(half_of(source, (h, opposite), 0), via.at[h, 0], 1, True),
+                    relay_b=step_copy(half_of(source, (h, opposite), 1), via.at[h, 1], 3, True),
                     direct_after=step_copy(
                         half_of(source, (h, after), 1), half_of(got, (h, 0), 1), 1
                     ),
@@ -379,21 +411,14 @@
         for step in STEPS:
             for p in range(3):
                 a = owner(p, 0, step)
-                build(p, h, a, 1 - c, outgoing[p].at[h, a])
+                build(p, a, 1 - c, outgoing[p].at[h, a])
                 pair_copies[h, p, step].start()
-
-    def build_own(h):
-        for step in STEPS:
-            for p in range(3):
-                a = owner(p, 0, step)
-                build(p, h, a, c, held[0][p].at[h, a])
 
     def join_partner(h, step):
         for p in range(3):
             a = owner(p, 0, step)
             pair_copies[h, p, step].wait_recv()
-            q = held[0][p].at[h, a]
-            add_blocks(q, (q, pair[p].at[h, a]))
+            build_joined(p, a, c, held[0][p].at[h, a], pair[p].at[h, a])
             if step == 2:
                 ring[h, 0, p]["relay_a"].start()
                 ring[h, 0, p]["relay_b"].start()
@@ -403,6 +428,11 @@
                 ring[h, 0, p]["direct_before"].start()
 
     def start_stage(h, stage):
+        if DIRECT[stage]:
+            for name in ("opposite", "after", "before"):
+                for p in range(3):
+                    ring[h, stage, p][name].start()
+            return
         for p in range(3):
             for name in ("relay_a", "relay_b"):
                 ring[h, stage, p][name].start()
@@ -411,6 +441,8 @@
                 ring[h, stage, p][name].start()
 
     def pass_on(h, stage):
+        if DIRECT[stage]:
+            return
         for p in range(3):
             source, via, copies = held[stage][p], relays[stage][p], ring[h, stage, p]
             copies["relay_a"].wait_recv()
@@ -428,39 +460,47 @@
     def finish_stage(h, stage):
         start = 0
         for p in range(3):
-            for name in ("direct_after", "direct_before", "summed_after", "summed_before"):
-                ring[h, stage, p][name].wait_recv()
             mine = held[stage][p].at[h, owner(p, stage, 0)]
             got = gots[stage][p]
+            arrival = ring_recv.at[ring[h, stage, p]["joint"]]
+            pltpu.make_async_copy(got.at[h], got.at[h], arrival).wait()
+            arrivals = range(3 if DIRECT[stage] else 2)
             if stage < 2:
-                add_blocks(held[stage + 1][p].at[h], (mine, got.at[h, 0], got.at[h, 1]))
+                add_blocks(held[stage + 1][p].at[h], (mine, *(got.at[h, i] for i in arrivals)))
             else:
                 at = pl.ds(h * ROWS, ROWS)
                 lanes = pl.ds(start, LANES[p])
-                out[at, lanes] = (
-                    mine[...] + got[h, 0] + got[h, 1] + self_term[at, lanes]
-                ).astype(BF)
+                value = mine[...].astype(F32) + self_term[at, lanes]
+                for i in arrivals:
+                    value += got[h, i].astype(F32)
+                out[at, lanes] = value.astype(BF)
                 start += LANES[p]
+
+    def wait_all_sent():
+        pltpu.make_async_copy(feats.at[pl.ds(0, 480)], feats.at[pl.ds(0, 480)], sent.at[0]).wait()
+        for p in range(3):
+            whole = outgoing[p]
+            pltpu.make_async_copy(whole, whole, sent.at[1 + p]).wait()
+            for stage in range(3):
+                whole = held[stage][p].at[:, pl.ds(0, RING - 1)]
+                pltpu.make_async_copy(whole, whole, sent.at[4 + stage * 3 + p]).wait()
 
     make_messages(0)
     add_tiles(0, 0, SLOTS)
     send_to_partner(0)
-    build_own(0)
+    make_messages(1)
     join_partner(0, 2)
-    make_messages(1)
+    make_self_term()
     for step in (1, 3, 0):
         join_partner(0, step)
     add_tiles(1, 0, 40)
     pass_on(0, 0)
     add_tiles(1, 40, SLOTS)
     send_to_partner(1)
-    build_own(1)
-    join_partner(1, 2)
+    for step in STEPS:
+        join_partner(1, step)
     finish_stage(0, 0)
     start_stage(0, 1)
-    for step in (1, 3, 0):
-        join_partner(1, step)
-    make_self_term()
     pass_on(0, 1)
     pass_on(1, 0)
     finish_stage(0, 1)
@@ -468,18 +508,16 @@
     finish_stage(1, 0)
     start_stage(1, 1)
     pass_on(0, 2)
+    finish_stage(0, 2)
     pass_on(1, 1)
-    finish_stage(0, 2)
     finish_stage(1, 1)
     start_stage(1, 2)
     pass_on(1, 2)
     finish_stage(1, 2)
-    for copies in (first, second, relay, pair_copies):
-        for copy in copies.values():
-            copy.wait_send()
-    for copies in ring.values():
-        for copy in copies.values():
-            copy.wait_send()
+    store = pltpu.make_async_copy(out, result, local.at[2])
+    store.start()
+    wait_all_sent()
+    store.wait()
 
 
 def body(node_feats, rel_weight, self_weight, bias, out_degree, adjacency, tile_index, tile_count):
@@ -490,8 +528,9 @@
         kernel,
         out_shape=jax.ShapeDtypeStruct((COLS, OWN), BF),
         in_specs=[VMEM, HBM, HBM, VMEM, VMEM, VMEM, SMEM, HBM],
-        out_specs=VMEM,
+        out_specs=HBM,
         scratch_shapes=[
+            pltpu.VMEM((COLS, OWN), BF),
             pltpu.VMEM((HID, OWN), BF),
             pltpu.VMEM((REL, HID, HID), BF),
             pltpu.VMEM((HID, HID), BF),
@@ -513,16 +552,14 @@
             *buffers(2, RING, RING),
             *buffers(RING, RING),
             *buffers(2, 2),
-            *buffers(2, RING),
+            *buffers(3 if DIRECT[1] else 2, RING),
             *buffers(RING, kind=F32),
             *buffers(2, kind=F32, rows=ROWS // 2),
-            *buffers(2, kind=F32),
-            pltpu.SemaphoreType.DMA((GATHER_COPIES,)),
-            pltpu.SemaphoreType.DMA((GATHER_COPIES,)),
-            pltpu.SemaphoreType.DMA((PAIR_COPIES,)),
-            pltpu.SemaphoreType.DMA((PAIR_COPIES,)),
-            pltpu.SemaphoreType.DMA((RING_COPIES,)),
-            pltpu.SemaphoreType.DMA((RING_COPIES,)),
+            *buffers(3 if DIRECT[2] else 2, kind=F32),
+            pltpu.SemaphoreType.DMA((13,)),
+            pltpu.SemaphoreType.DMA((GATHER_ARRIVALS,)),
+            pltpu.SemaphoreType.DMA((PAIR_ARRIVALS,)),
+            pltpu.SemaphoreType.DMA((RING_ARRIVALS,)),
             pltpu.SemaphoreType.DMA((3,)),
             pltpu.SemaphoreType.DMA((DEPTH,)),
         ],

time: 72.4 us -> 57.7 us (0.80)
  Pallas kernels: 70 us -> 55.2 us
    pallas_call x1, Pallas kernels: 70 us -> 55.2 us  [body(): pl.pallas_call(kernel, out_shape=jax.ShapeDtypeStruct((COLS, OWN), BF), i...]
where the time goes in v3:
time: 57.7 us; the launch traced here: 57.3 us
  Pallas kernels  55.2 us (96%)
  local copies, waits for them, and re-layouts  1.47 us (3%)
  between operations  0.66 us (1%)
    pallas_call x1, Pallas kernels, body(): pl.pallas_call(kernel, out_shape=jax.ShapeDtypeStruct((COLS, OWN), BF), i...  55.2 us
    unnamed x1, local copies, waits for them, and re-layouts  1.47 us

profile of v3, /device:TPU:0, one launch (start us, length us, event | category | flops | bytes accessed | tf_op | source)
XLA Modules:
  0.0 57.3 jit_solution(16706019267735302533)
XLA Ops:
  0.7 55.2 %relational_layer.1 = bf16[32,1024]{1,0:T(8,128)(2,1)} custom-call(bf16[32,1024]{1,0:T(8,128)(2,1)} %bitcast.9, bf16[4,512,512]{2,1,0:T(8,128)(2,1)} %rel.1, bf16[512,512]{1,0:T(8,128)(2,1)} %own.1, f32[1,512]{1,0:T(1,128)} %bitcast.10, s32[4,1024]{1,0:T(4,128)} %degree.1, s32[3,1,64]{2,1,0:T(1,128)} %bitcast.11, s32[1,1]{1,0:T(1,128)S(6)} %copy.10.live, ...), custom_call_target="tpu_custom_call" | custom-call | tf_op jit(solution)/shard_map/relational_layer/pallas_call | solution.py:527
  55.9 1.5 %copy.11 = bf16[1024,32]{0,1:T(8,128)(2,1)} copy(bf16[1024,32]{0,1:T(8,128)(2,1)} %bitcast.8) | data formatting | bytes 131072

commit v4 on v2

v4 whole, which is shorter than its diff:
```python
import jax
import jax.numpy as jnp
from jax import lax
from jax.experimental import pallas as pl
from jax.experimental.pallas import tpu as pltpu
from jax.sharding import PartitionSpec as P

MESH = pl.DeviceIdType.MESH
BF = jnp.bfloat16
F32 = jnp.float32
I32 = jnp.int32
RING = 4
HID = 512
COLS = 32
ROWS = 8
OWN = 1024
TILE = 256
SLOTS = 64
REL = 4
BLOCKS = 32
HALVES = 2
PIECES = 4
BATCH = 4
DEPTH = 8
UNROLL = 32
LANES = (384, 384, 256)
ORDER = ("xyz", "yzx", "zxy")
STEPS = (2, 1, 3, 0)
VMEM = pl.BlockSpec(memory_space=pltpu.VMEM)
SMEM = pl.BlockSpec(memory_space=pltpu.SMEM)
HBM = pl.BlockSpec(memory_space=pl.ANY)
NT = (((1,), (1,)), ((), ()))
GATHER_ARRIVALS = 2 * 3 + 1
PAIR_ARRIVALS = PIECES * 4
RING_ARRIVALS = PIECES * 9


def place():
    dom = lax.axis_index("dom")
    feat = lax.axis_index("feat")
    return dict(z=dom // 2, c=dom % 2, x=feat // RING, y=feat % RING)


def device(here, **moved):
    at = dict(here)
    for axis, step in moved.items():
        at[axis] = (at[axis] + step) % (2 if axis == "c" else RING)
    return (at["z"] * 2 + at["c"], at["x"] * RING + at["y"])


def greet(peers):
    barrier = pltpu.get_barrier_semaphore()
    for peer in peers:
        pl.semaphore_signal(barrier, inc=1, device_id=peer, device_id_type=MESH)
    pl.semaphore_wait(barrier, len(peers))


def aligned(start, size):
    return pl.ds(pl.multiple_of(start, size), size)


def sort_slots(index, live, table):
    shape = (128, 128)
    across = lax.broadcasted_iota(I32, shape, 1)
    down = lax.broadcasted_iota(I32, shape, 0)

    def row(value):
        return jnp.broadcast_to(jnp.concatenate([value, value], axis=1), shape)

    is_live = across < live
    target = jnp.where(is_live, row(index[1]), BLOCKS)
    block = row(index[0]) * 4 + row(index[2])
    key = jnp.where(across < SLOTS, target * 128 + across, 65536 + across)
    key_down = key.T
    rank = jnp.sum(jnp.where(key_down < key, 1, 0), axis=0, keepdims=True)
    rank_down = jnp.broadcast_to(rank, shape).T
    hit = rank_down == across
    target_down = target.T
    table[0:1, :] = jnp.sum(jnp.where(hit, down, 0), axis=0, keepdims=True)
    table[1:2, :] = jnp.sum(jnp.where(hit, block.T, 0), axis=0, keepdims=True)
    table[2:3, :] = jnp.sum(jnp.where(hit, target_down, 0), axis=0, keepdims=True)
    real = down < SLOTS
    upto = jnp.sum(jnp.where(real & (target_down <= across), 1, 0), axis=0, keepdims=True)
    below = jnp.sum(jnp.where(real & (target_down < across), 1, 0), axis=0, keepdims=True)
    table[3:4, :] = jnp.where(upto > below, upto, 0)


def kernel(
    nodes, rel, own, bias_hbm, degree_hbm, index_hbm, live, tiles, result,
    bias, degree, index, out,    feats, rel_in, own_in, rel_t, own_t, bias_t, self_term, inverse, msg,
    raw, cells, sums, table, order,
    out_x, out_y, out_z, pair_x, pair_y, pair_z,
    relay_x, relay_y, relay_z, got1x, got1y, got1z,
    q2x, q2y, q2z, got2x, got2y, got2z, q3x, q3y, q3z, got3x, got3y, got3z,
    sent, gather_recv, pair_recv, ring_recv, local, arrived,
):
    here = place()
    outgoing = (out_x, out_y, out_z)
    pair = (pair_x, pair_y, pair_z)
    relays = (relay_x, relay_y, relay_z)
    got1, got2, got3 = (got1x, got1y, got1z), (got2x, got2y, got2z), (got3x, got3y, got3z)
    q2, q3 = (q2x, q2y, q2z), (q3x, q3y, q3z)
    c = here["c"]

    mine = aligned((here["x"] * RING + here["y"]) * COLS, COLS)
    fetch_nodes = pltpu.make_async_copy(nodes, feats.at[mine, :], local.at[3])
    fetch_nodes.start()
    fetch_small = [
        pltpu.make_async_copy(src, dst, local.at[4 + i])
        for i, (src, dst) in enumerate(((index_hbm, index), (degree_hbm, degree), (bias_hbm, bias)))
    ]
    for fetch in fetch_small:
        fetch.start()
    fetch_rel = pltpu.make_async_copy(rel, rel_in, local.at[0])
    fetch_own = pltpu.make_async_copy(own, own_in, local.at[1])
    fetch_rel.start()
    fetch_own.start()

    def fetch_tiles(batch, slot):
        return pltpu.make_async_copy(
            tiles.at[pl.ds(batch * BATCH, BATCH)], raw.at[slot], arrived.at[slot]
        )

    for batch in range(DEPTH):
        fetch_tiles(batch, batch).start()
    partner = device(here, c=1)
    peers = [device(here, **{axis: step}) for axis in "xy" for step in (1, 2, 3)]
    peers += [device(here, z=step) for step in (1, 3)] + [partner]
    greet(peers)

    half = COLS // 2
    first_axis = ("x", "y")
    second_axis = ("y", "x")

    def rows(h, x, y):
        return aligned((x * RING + y) * COLS + h * half, half)

    counts = dict(gather=0)

    def remote(src, dst, peer, arrival=None):
        if arrival is None:
            arrival = counts["gather"]
            counts["gather"] += 1
        return pltpu.make_async_remote_copy(
            src_ref=src, dst_ref=dst, send_sem=sent.at[0], recv_sem=gather_recv.at[arrival],
            device_id=peer, device_id_type=MESH,
        )

    def part(h, a, b, lanes=pl.ds(0, OWN)):
        moved = {first_axis[h]: a, second_axis[h]: b}
        at = rows(h, (here["x"] + moved["x"]) % RING, (here["y"] + moved["y"]) % RING)
        return feats.at[at, lanes]

    fetch_nodes.wait()
    first, second = {}, {}
    for h in (0, 1):
        src = part(h, 0, 0)
        for step in (1, 3, 2):
            first[h, step] = remote(src, part(h, 0, 0), device(here, **{first_axis[h]: step}))
        for a in (0, 1, 3, 2):
            for step in (1, 3, 2):
                second[h, a, step] = remote(
                    part(h, a, 0), part(h, a, 0),
                    device(here, **{second_axis[h]: step}), GATHER_ARRIVALS - 1,
                )
    for step in (1, 3, 2):
        for h in (0, 1):
            first[h, step].start()
    for step in (2, 1, 3):
        for h in (0, 1):
            second[h, 0, step].start()

    def forward(a):
        for h in (0, 1):
            first[h, RING - a].wait_recv()
            for step in (2, 1, 3):
                second[h, a, step].start()

    def transpose(r):
        turned = rel_in[r].astype(F32).T.reshape(HID // COLS, HALVES, 2, ROWS, HID)
        for h in range(HALVES):
            for i in range(2):
                some = turned[:, h, i].reshape(HID // PIECES, HID)
                rel_t[r, h, pl.ds(i * (HID // PIECES), HID // PIECES), :] = some.astype(BF)

    def convert(low, high):
        def one(batch, carry):
            slot = batch % DEPTH
            fetch_tiles(batch, slot).wait()

            def tile(i, carry):
                cells[batch * BATCH + i] = raw[slot, i].astype(F32).astype(BF)
                return carry

            lax.fori_loop(0, BATCH, tile, 0, unroll=2)

            @pl.when(batch + DEPTH < SLOTS // BATCH)
            def _():
                fetch_tiles(batch + DEPTH, slot).start()

            return carry

        lax.fori_loop(low, high, one, 0)

    for fetch in fetch_small:
        fetch.wait()
    inverse[...] = 1.0 / jnp.maximum(degree[...], 1).astype(F32)
    sort_slots(index, live[0, 0], table)
    fetch_order = pltpu.make_async_copy(table, order, local.at[2])
    fetch_order.start()
    sums[0] = jnp.zeros((HID // 2, TILE), F32)
    fetch_rel.wait()
    fetch_own.wait()
    for r in range(REL):
        transpose(r)
    convert(0, 6)
    forward(3)
    forward(1)
    forward(2)
    own_t[...] = own_in[...].T
    bias_t[...] = jnp.broadcast_to(bias[...], (128, HID)).T
    convert(6, SLOTS // BATCH)
    fetch_order.wait()
    rest = feats.at[pl.ds(0, 384)]
    pltpu.make_async_copy(rest, rest, gather_recv.at[GATHER_ARRIVALS - 1]).wait()

    def make_messages(h, sources):
        for s in sources:
            at = pl.ds(s * TILE, TILE)

            def relation(r, carry):
                product = jnp.dot(rel_t[r, h], feats[:, at], preferred_element_type=F32)
                msg[h, r * 4 + s] = (product * inverse[pl.ds(r, 1), at]).astype(BF)
                return carry

            lax.fori_loop(0, REL, relation, 0, unroll=True)

    def make_self_term():
        bias_rows = bias_t[mine, :]
        for s in range(OWN // TILE):
            at = pl.ds(s * TILE, TILE)
            self_term[:, at] = jnp.dot(
                own_t[mine, :], feats[:, at], preferred_element_type=F32
            ) + jnp.concatenate([bias_rows, bias_rows], axis=1)

    def add_tiles(h, low, high):
        def some(i, carry):
            for u in range(UNROLL):
                t = i * UNROLL + u
                product = lax.dot_general(
                    msg[h, order[1, t]], cells[order[0, t]], NT, preferred_element_type=F32
                )
                before = order[2, jnp.maximum(t - 1, 0)]
                same = jnp.where((t > 0) & (order[2, t] == before), 1.0, 0.0)
                sums[t + 1] = sums[t] * same + product
            return carry

        lax.fori_loop(low // UNROLL, high // UNROLL, some, 0)

    def owner(p, stage, step):
        return (here[ORDER[p][stage]] + step) % RING

    def blocks(k, p, a, core):
        start = k % 2 * (HID // PIECES)

        def at(x, y):
            return aligned(start + (x * RING + y) * ROWS, ROWS)

        def last(z, b):
            return order[3, z * 8 + core * 4 + b]

        if p == 2:
            for x in range(RING):
                rows = aligned(start + x * RING * ROWS, RING * ROWS)
                yield x, pl.ds(0, 256), sums[last(a, 3), rows, :]
            return
        for m in range(RING):
            if p == 0:
                one = [sums[last(z, 0), at(a, m), :] for z in range(RING)]
                two = [sums[last(z, 1), at(a, m), 0:128] for z in range(RING)]
            else:
                one = [sums[last(m, 1), at(x, a), 128:256] for x in range(RING)]
                two = [sums[last(m, 2), at(x, a), :] for x in range(RING)]
            width = one[0].shape[1]
            yield m, pl.ds(0, width), jnp.concatenate(one, axis=0)
            yield m, pl.ds(width, 384 - width), jnp.concatenate(two, axis=0)

    def await_bytes(ref, semaphore):
        pltpu.make_async_copy(ref, ref, semaphore).wait()

    pair_copies = {}
    for k in range(PIECES):
        for n, step in enumerate(STEPS):
            for p in range(3):
                a = owner(p, 0, step)
                pair_copies[k, p, step] = pltpu.make_async_remote_copy(
                    src_ref=outgoing[p].at[k, a], dst_ref=pair[p].at[k, a],
                    send_sem=sent.at[1], recv_sem=pair_recv.at[k * 4 + n],
                    device_id=partner, device_id_type=MESH,
                )

    def half_of(ref, lead, which):
        n = ref.shape[len(lead)] // 2
        return ref.at[(*lead, pl.ds(which * n, n))]

    ring = {}
    for k in range(PIECES):
        for p in range(3):

            def step_copy(stage, src, dst, step, arrival):
                return pltpu.make_async_remote_copy(
                    src_ref=src, dst_ref=dst, send_sem=sent.at[2 + stage],
                    recv_sem=ring_recv.at[k * 9 + arrival],
                    device_id=device(here, **{ORDER[p][stage]: step}), device_id_type=MESH,
                )

            opposite, after, before = (owner(p, 0, step) for step in (2, 1, 3))
            source, via, got = pair[p], relays[p], got1[p]
            ring[k, 0, p] = dict(
                relay_a=step_copy(0, half_of(source, (k, opposite), 0), via.at[k, 0], 1, 3 + p),
                relay_b=step_copy(0, half_of(source, (k, opposite), 1), via.at[k, 1], 3, 6 + p),
                direct_after=step_copy(
                    0, half_of(source, (k, after), 1), half_of(got, (k, 0), 1), 1, 0
                ),
                direct_before=step_copy(
                    0, half_of(source, (k, before), 0), half_of(got, (k, 1), 0), 3, 0
                ),
                summed_after=step_copy(
                    0, half_of(source, (k, after), 0), half_of(got, (k, 0), 0), 1, 0
                ),
                summed_before=step_copy(
                    0, half_of(source, (k, before), 1), half_of(got, (k, 1), 1), 3, 0
                ),
            )
            ring[k, 1, p] = [
                step_copy(1, q2[p].at[k, owner(p, 1, step)], got2[p].at[k, i], step, 1)
                for i, step in enumerate((2, 1, 3))
            ]
            ring[k, 2, p] = [
                step_copy(
                    2, q3[p].at[k, aligned(owner(p, 2, step) * ROWS, ROWS)], got3[p].at[k, i], step, 2
                )
                for i, step in enumerate((2, 1, 3))
            ]

    def send_to_partner(k, step):
        for p in range(3):
            a = owner(p, 0, step)
            for m, lanes, value in blocks(k, p, a, 1 - c):
                out_p = outgoing[p]
                out_p[k, a, m, :, lanes] = value.astype(BF)
            pair_copies[k, p, step].start()

    def join_partner(k, step):
        await_bytes(msg.at[0, pl.ds(0, 2)], pair_recv.at[k * 4 + STEPS.index(step)])
        for p in range(3):
            a = owner(p, 0, step)
            for m, lanes, value in blocks(k, p, a, c):
                arrived_p = pair[p]
                arrived_p[k, a, m, :, lanes] = (
                    value + arrived_p[k, a, m, :, lanes].astype(F32)
                ).astype(BF)
            if step == 2:
                ring[k, 0, p]["relay_a"].start()
                ring[k, 0, p]["relay_b"].start()
            elif step == 1:
                ring[k, 0, p]["direct_after"].start()
            elif step == 3:
                ring[k, 0, p]["direct_before"].start()

    def start_stage(k, stage):
        for i in range(3):
            for p in range(3):
                ring[k, stage, p][i].start()

    def add_into(dst, sources):
        for i in range(dst.shape[0]):
            value = sources[0][i].astype(F32)
            for source in sources[1:]:
                value += source[i].astype(F32)
            dst[i] = value.astype(dst.dtype)

    def pass_on(k):
        for p in range(3):
            source, via = pair[p], relays[p]
            await_bytes(via.at[k, 0], ring_recv.at[k * 9 + 3 + p])
            mine = half_of(source, (k, owner(p, 0, 1)), 0)
            add_into(mine, (mine, via.at[k, 0]))
            ring[k, 0, p]["summed_after"].start()
            await_bytes(via.at[k, 1], ring_recv.at[k * 9 + 6 + p])
            mine = half_of(source, (k, owner(p, 0, 3)), 1)
            add_into(mine, (mine, via.at[k, 1]))
            ring[k, 0, p]["summed_before"].start()

    def finish_first(k):
        await_bytes(feats.at[pl.ds(0, 256)], ring_recv.at[k * 9])
        for p in range(3):
            mine = pair[p].at[k, owner(p, 0, 0)]
            add_into(q2[p].at[k], (mine, got1[p].at[k, 0], got1[p].at[k, 1]))
        start_stage(k, 1)

    def finish_second(k):
        await_bytes(feats.at[pl.ds(0, 96)], ring_recv.at[k * 9 + 1])
        for p in range(3):
            value = q2[p][k, owner(p, 1, 0)].astype(F32)
            for i in range(3):
                value += got2[p][k, i].astype(F32)
            q3[p][k] = value
        start_stage(k, 2)

    def finish_third(k):
        await_bytes(feats.at[pl.ds(0, 48)], ring_recv.at[k * 9 + 2])
        start = 0
        at = pl.ds(k * ROWS, ROWS)
        for p in range(3):
            lanes = pl.ds(start, LANES[p])
            value = q3[p][k, aligned(owner(p, 2, 0) * ROWS, ROWS), :] + self_term[at, lanes]
            for i in range(3):
                value += got3[p][k, i]
            out[at, lanes] = value.astype(BF)
            start += LANES[p]

    def wait_all_sent():
        await_bytes(feats.at[pl.ds(0, 480)], sent.at[0])
        await_bytes(msg, sent.at[1])
        await_bytes(msg.at[:, pl.ds(0, 12)], sent.at[2])
        await_bytes(feats.at[pl.ds(0, 384)], sent.at[3])
        await_bytes(feats.at[pl.ds(0, 192)], sent.at[4])

    SEND = ((0, 2), (1, 2), (0, 1), (0, 3), (1, 1), (1, 3), (0, 0), (1, 0))

    make_messages(0, range(4))
    add_tiles(0, 0, SLOTS)
    for k, step in SEND:
        send_to_partner(k, step)
    make_messages(1, range(2))
    join_partner(0, 2)
    join_partner(1, 2)
    make_messages(1, range(2, 4))
    make_self_term()
    for k, step in SEND[2:]:
        join_partner(k, step)
    add_tiles(1, 0, 32)
    pass_on(0)
    pass_on(1)
    add_tiles(1, 32, SLOTS)
    for k, step in SEND:
        send_to_partner(2 + k, step)
    for k, step in SEND:
        join_partner(2 + k, step)
    pass_on(2)
    pass_on(3)
    for k in range(PIECES):
        finish_first(k)
    for k in range(PIECES):
        finish_second(k)
    for k in range(PIECES):
        finish_third(k)
    store = pltpu.make_async_copy(out, result, local.at[2])
    store.start()
    wait_all_sent()
    store.wait()


def body(node_feats, rel_weight, self_weight, bias, out_degree, adjacency, tile_index, tile_count):
    def buffers(*lead, kind=BF, rows=RING * ROWS):
        return [pltpu.VMEM((PIECES, *lead, rows, lanes), kind) for lanes in LANES]

    result = pl.pallas_call(
        kernel,
        out_shape=jax.ShapeDtypeStruct((COLS, OWN), BF),
        in_specs=[HBM, HBM, HBM, HBM, HBM, HBM, SMEM, HBM],
        out_specs=HBM,
        scratch_shapes=[
            pltpu.VMEM((1, HID), F32),
            pltpu.VMEM((REL, OWN), I32),
            pltpu.VMEM((3, 1, SLOTS), I32),
            pltpu.VMEM((COLS, OWN), BF),
            pltpu.VMEM((HID, OWN), BF),
            pltpu.VMEM((REL, HID, HID), BF),
            pltpu.VMEM((HID, HID), BF),
            pltpu.VMEM((REL, HALVES, HID // 2, HID), BF),
            pltpu.VMEM((HID, HID), BF),
            pltpu.VMEM((HID, 128), F32),
            pltpu.VMEM((COLS, OWN), F32),
            pltpu.VMEM((REL, OWN), F32),
            pltpu.VMEM((HALVES, REL * 4, HID // 2, TILE), BF),
            pltpu.VMEM((DEPTH, BATCH, TILE, TILE), I32),
            pltpu.VMEM((SLOTS, TILE, TILE), BF),
            pltpu.VMEM((SLOTS + 1, HID // 2, TILE), F32),
            pltpu.VMEM((8, 128), I32),
            pltpu.SMEM((8, 128), I32),
            *buffers(RING, RING),
            *buffers(RING, RING),
            *buffers(2, 2),
            *buffers(2, RING),
            *buffers(RING),
            *buffers(3),
            *buffers(kind=F32),
            *buffers(3, kind=F32, rows=ROWS),
            pltpu.SemaphoreType.DMA((5,)),
            pltpu.SemaphoreType.DMA((GATHER_ARRIVALS,)),
            pltpu.SemaphoreType.DMA((PAIR_ARRIVALS,)),
            pltpu.SemaphoreType.DMA((RING_ARRIVALS,)),
            pltpu.SemaphoreType.DMA((7,)),
            pltpu.SemaphoreType.DMA((DEPTH,)),
        ],
        compiler_params=pltpu.CompilerParams(
            collective_id=0, has_side_effects=True, vmem_limit_bytes=63 * 2**20
        ),
        name="relational_layer",
    )(
        node_feats.T, rel_weight, self_weight, bias.reshape(1, HID), out_degree,
        jnp.transpose(tile_index[0], (2, 0, 1)), tile_count, adjacency[0, 0],
    )
    return result.T


def solution(mesh):
    placed = (
        P("dom", "feat"),
        P(),
        P(),
        P(),
        P(None, "dom"),
        P("dom", "feat", None, None, None),
        P("dom", "feat", None, None),
        P("dom", "feat"),
    )
    return jax.shard_map(
        body, mesh=mesh, in_specs=placed, out_specs=P("dom", "feat"), check_vma=False
    )
```

time: 72.4 us -> 51.4 us (0.71)
  Pallas kernels: 70 us -> 49.1 us
    pallas_call x1, Pallas kernels: 70 us -> 49.1 us  [body(): pl.pallas_call(kernel, out_shape=jax.ShapeDtypeStruct((COLS, OWN), BF), i...]
where the time goes in v4:
time: 51.4 us; the launch traced here: 51.2 us
  Pallas kernels  49.1 us (96%)
  local copies, waits for them, and re-layouts  1.47 us (3%)
  between operations  0.66 us (1%)
    pallas_call x1, Pallas kernels, body(): pl.pallas_call(kernel, out_shape=jax.ShapeDtypeStruct((COLS, OWN), BF), i...  49.1 us
    unnamed x1, local copies, waits for them, and re-layouts  1.47 us

profile of v4, /device:TPU:0, one launch (start us, length us, event | category | flops | bytes accessed | tf_op | source)
XLA Modules:
  0.0 51.2 jit_solution(18076212867885681247)
XLA Ops:
  0.7 49.1 %relational_layer.1 = bf16[32,1024]{1,0:T(8,128)(2,1)} custom-call(bf16[32,1024]{1,0:T(8,128)(2,1)} %bitcast.9, bf16[4,512,512]{2,1,0:T(8,128)(2,1)} %rel.1, bf16[512,512]{1,0:T(8,128)(2,1)} %own.1, f32[1,512]{1,0:T(1,128)} %bitcast.10, s32[4,1024]{1,0:T(4,128)} %degree_hbm.1, s32[3,1,64]{2,1,0:T(1,128)} %bitcast.11, s32[1,1]{1,0:T(1,128)S(6)} %copy.10.live, ...), custom_call_target="tpu_custom_call" | custom-call | tf_op jit(solution)/shard_map/relational_layer/pallas_call | solution.py:469
  49.7 1.5 %copy.11 = bf16[1024,32]{0,1:T(8,128)(2,1)} copy(bf16[1024,32]{0,1:T(8,128)(2,1)} %bitcast.8) | data formatting | bytes 131072

commit v5 on v4

--- a/solution.py
+++ b/solution.py
@@ -32,7 +32,7 @@
 NT = (((1,), (1,)), ((), ()))
 GATHER_ARRIVALS = 2 * 3 + 1
 PAIR_ARRIVALS = PIECES * 4
-RING_ARRIVALS = PIECES * 9
+RING_ARRIVALS = PIECES * 5
 
 
 def place():
@@ -135,46 +135,40 @@
     def rows(h, x, y):
         return aligned((x * RING + y) * COLS + h * half, half)
 
-    counts = dict(gather=0)
-
-    def remote(src, dst, peer, arrival=None):
-        if arrival is None:
-            arrival = counts["gather"]
-            counts["gather"] += 1
+
+    def remote(src, dst, peer, arrival):
         return pltpu.make_async_remote_copy(
             src_ref=src, dst_ref=dst, send_sem=sent.at[0], recv_sem=gather_recv.at[arrival],
             device_id=peer, device_id_type=MESH,
         )
 
-    def part(h, a, b, lanes=pl.ds(0, OWN)):
-        moved = {first_axis[h]: a, second_axis[h]: b}
-        at = rows(h, (here["x"] + moved["x"]) % RING, (here["y"] + moved["y"]) % RING)
-        return feats.at[at, lanes]
+    def part(h, a):
+        at = dict(here)
+        at[first_axis[h]] = (at[first_axis[h]] + a) % RING
+        return feats.at[rows(h, at["x"], at["y"]), :]
 
     fetch_nodes.wait()
-    first, second = {}, {}
-    for h in (0, 1):
-        src = part(h, 0, 0)
-        for step in (1, 3, 2):
-            first[h, step] = remote(src, part(h, 0, 0), device(here, **{first_axis[h]: step}))
-        for a in (0, 1, 3, 2):
-            for step in (1, 3, 2):
-                second[h, a, step] = remote(
-                    part(h, a, 0), part(h, a, 0),
-                    device(here, **{second_axis[h]: step}), GATHER_ARRIVALS - 1,
-                )
     for step in (1, 3, 2):
         for h in (0, 1):
-            first[h, step].start()
-    for step in (2, 1, 3):
+            peer = device(here, **{first_axis[h]: step})
+            remote(part(h, 0), part(h, 0), peer, h * 3 + RING - step - 1).start()
+
+    def spread(h, a):
+        for step in (2, 1, 3):
+            peer = device(here, **{second_axis[h]: step})
+            remote(part(h, a), part(h, a), peer, GATHER_ARRIVALS - 1).start()
+
+    for h in (0, 1):
+        spread(h, 0)
+
+    def forward(i):
         for h in (0, 1):
-            second[h, 0, step].start()
-
-    def forward(a):
-        for h in (0, 1):
-            first[h, RING - a].wait_recv()
-            for step in (2, 1, 3):
-                second[h, a, step].start()
+            at = here[first_axis[h]]
+            other = i + jnp.where(at <= i, 1, 0)
+            a = (other - at + RING) % RING
+            piece = part(h, a)
+            pltpu.make_async_copy(piece, piece, gather_recv.at[h * 3 + a - 1]).wait()
+            spread(h, a)
 
     def transpose(r):
         turned = rel_in[r].astype(F32).T.reshape(HID // COLS, HALVES, 2, ROWS, HID)
@@ -214,7 +208,7 @@
     for r in range(REL):
         transpose(r)
     convert(0, 6)
-    forward(3)
+    forward(0)
     forward(1)
     forward(2)
     own_t[...] = own_in[...].T
@@ -243,10 +237,10 @@
                 own_t[mine, :], feats[:, at], preferred_element_type=F32
             ) + jnp.concatenate([bias_rows, bias_rows], axis=1)
 
-    def add_tiles(h, low, high):
+    def add_tiles(h, low, high, unroll=UNROLL):
         def some(i, carry):
-            for u in range(UNROLL):
-                t = i * UNROLL + u
+            for u in range(unroll):
+                t = i * unroll + u
                 product = lax.dot_general(
                     msg[h, order[1, t]], cells[order[0, t]], NT, preferred_element_type=F32
                 )
@@ -255,7 +249,7 @@
                 sums[t + 1] = sums[t] * same + product
             return carry
 
-        lax.fori_loop(low // UNROLL, high // UNROLL, some, 0)
+        lax.fori_loop(low // unroll, high // unroll, some, 0)
 
     def owner(p, stage, step):
         return (here[ORDER[p][stage]] + step) % RING
@@ -310,15 +304,15 @@
             def step_copy(stage, src, dst, step, arrival):
                 return pltpu.make_async_remote_copy(
                     src_ref=src, dst_ref=dst, send_sem=sent.at[2 + stage],
-                    recv_sem=ring_recv.at[k * 9 + arrival],
+                    recv_sem=ring_recv.at[k * 5 + arrival],
                     device_id=device(here, **{ORDER[p][stage]: step}), device_id_type=MESH,
                 )
 
             opposite, after, before = (owner(p, 0, step) for step in (2, 1, 3))
             source, via, got = pair[p], relays[p], got1[p]
             ring[k, 0, p] = dict(
-                relay_a=step_copy(0, half_of(source, (k, opposite), 0), via.at[k, 0], 1, 3 + p),
-                relay_b=step_copy(0, half_of(source, (k, opposite), 1), via.at[k, 1], 3, 6 + p),
+                relay_a=step_copy(0, half_of(source, (k, opposite), 0), via.at[k, 0], 1, 3),
+                relay_b=step_copy(0, half_of(source, (k, opposite), 1), via.at[k, 1], 3, 4),
                 direct_after=step_copy(
                     0, half_of(source, (k, after), 1), half_of(got, (k, 0), 1), 1, 0
                 ),
@@ -381,26 +375,22 @@
             dst[i] = value.astype(dst.dtype)
 
     def pass_on(k):
-        for p in range(3):
-            source, via = pair[p], relays[p]
-            await_bytes(via.at[k, 0], ring_recv.at[k * 9 + 3 + p])
-            mine = half_of(source, (k, owner(p, 0, 1)), 0)
-            add_into(mine, (mine, via.at[k, 0]))
-            ring[k, 0, p]["summed_after"].start()
-            await_bytes(via.at[k, 1], ring_recv.at[k * 9 + 6 + p])
-            mine = half_of(source, (k, owner(p, 0, 3)), 1)
-            add_into(mine, (mine, via.at[k, 1]))
-            ring[k, 0, p]["summed_before"].start()
+        for way, step, name in ((0, 1, "summed_after"), (1, 3, "summed_before")):
+            await_bytes(feats.at[pl.ds(0, 64)], ring_recv.at[k * 5 + 3 + way])
+            for p in range(3):
+                mine = half_of(pair[p], (k, owner(p, 0, step)), way)
+                add_into(mine, (mine, relays[p].at[k, way]))
+                ring[k, 0, p][name].start()
 
     def finish_first(k):
-        await_bytes(feats.at[pl.ds(0, 256)], ring_recv.at[k * 9])
+        await_bytes(feats.at[pl.ds(0, 256)], ring_recv.at[k * 5])
         for p in range(3):
             mine = pair[p].at[k, owner(p, 0, 0)]
             add_into(q2[p].at[k], (mine, got1[p].at[k, 0], got1[p].at[k, 1]))
         start_stage(k, 1)
 
     def finish_second(k):
-        await_bytes(feats.at[pl.ds(0, 96)], ring_recv.at[k * 9 + 1])
+        await_bytes(feats.at[pl.ds(0, 96)], ring_recv.at[k * 5 + 1])
         for p in range(3):
             value = q2[p][k, owner(p, 1, 0)].astype(F32)
             for i in range(3):
@@ -409,7 +399,7 @@
         start_stage(k, 2)
 
     def finish_third(k):
-        await_bytes(feats.at[pl.ds(0, 48)], ring_recv.at[k * 9 + 2])
+        await_bytes(feats.at[pl.ds(0, 48)], ring_recv.at[k * 5 + 2])
         start = 0
         at = pl.ds(k * ROWS, ROWS)
         for p in range(3):
@@ -437,17 +427,19 @@
     join_partner(0, 2)
     join_partner(1, 2)
     make_messages(1, range(2, 4))
-    make_self_term()
     for k, step in SEND[2:]:
         join_partner(k, step)
-    add_tiles(1, 0, 32)
+    add_tiles(1, 0, 48, 24)
     pass_on(0)
+    add_tiles(1, 48, SLOTS, 16)
+    for k, step in SEND[:2]:
+        send_to_partner(2 + k, step)
     pass_on(1)
-    add_tiles(1, 32, SLOTS)
-    for k, step in SEND:
+    for k, step in SEND[2:]:
         send_to_partner(2 + k, step)
     for k, step in SEND:
         join_partner(2 + k, step)
+    make_self_term()
     pass_on(2)
     pass_on(3)
     for k in range(PIECES):

time: 51.4 us -> 49.8 us (0.969)
  Pallas kernels: 49.1 us -> 47.5 us
    pallas_call x1, Pallas kernels: 49.1 us -> 47.5 us  [body(): pl.pallas_call(kernel, out_shape=jax.ShapeDtypeStruct((COLS, OWN), BF), i...]
where the time goes in v5:
time: 49.8 us; the launch traced here: 49.6 us
  Pallas kernels  47.5 us (95%)
  local copies, waits for them, and re-layouts  1.47 us (3%)
  between operations  0.66 us (1%)
    pallas_call x1, Pallas kernels, body(): pl.pallas_call(kernel, out_shape=jax.ShapeDtypeStruct((COLS, OWN), BF), i...  47.5 us
    unnamed x1, local copies, waits for them, and re-layouts  1.47 us

profile of v5, /device:TPU:0, one launch (start us, length us, event | category | flops | bytes accessed | tf_op | source)
XLA Modules:
  0.0 49.6 jit_solution(269663753273089595)
XLA Ops:
  0.7 47.5 %relational_layer.1 = bf16[32,1024]{1,0:T(8,128)(2,1)} custom-call(bf16[32,1024]{1,0:T(8,128)(2,1)} %bitcast.9, bf16[4,512,512]{2,1,0:T(8,128)(2,1)} %rel.1, bf16[512,512]{1,0:T(8,128)(2,1)} %own.1, f32[1,512]{1,0:T(1,128)} %bitcast.10, s32[4,1024]{1,0:T(4,128)} %degree_hbm.1, s32[3,1,64]{2,1,0:T(1,128)} %bitcast.11, s32[1,1]{1,0:T(1,128)S(6)} %copy.10.live, ...), custom_call_target="tpu_custom_call" | custom-call | tf_op jit(solution)/shard_map/relational_layer/pallas_call | solution.py:461
  48.2 1.5 %copy.11 = bf16[1024,32]{0,1:T(8,128)(2,1)} copy(bf16[1024,32]{0,1:T(8,128)(2,1)} %bitcast.8) | data formatting | bytes 131072

commit v6 on v5

--- a/solution.py
+++ b/solution.py
@@ -31,7 +31,7 @@
 HBM = pl.BlockSpec(memory_space=pl.ANY)
 NT = (((1,), (1,)), ((), ()))
 GATHER_ARRIVALS = 2 * 3 + 1
-PAIR_ARRIVALS = PIECES * 4
+PAIR_ARRIVALS = PIECES * 6
 RING_ARRIVALS = PIECES * 5
 
 
@@ -268,16 +268,20 @@
                 rows = aligned(start + x * RING * ROWS, RING * ROWS)
                 yield x, pl.ds(0, 256), sums[last(a, 3), rows, :]
             return
-        for m in range(RING):
-            if p == 0:
-                one = [sums[last(z, 0), at(a, m), :] for z in range(RING)]
-                two = [sums[last(z, 1), at(a, m), 0:128] for z in range(RING)]
-            else:
-                one = [sums[last(m, 1), at(x, a), 128:256] for x in range(RING)]
-                two = [sums[last(m, 2), at(x, a), :] for x in range(RING)]
-            width = one[0].shape[1]
-            yield m, pl.ds(0, width), jnp.concatenate(one, axis=0)
-            yield m, pl.ds(width, 384 - width), jnp.concatenate(two, axis=0)
+        if p == 0:
+            rows = aligned(start + a * RING * ROWS, RING * ROWS)
+            for b, lanes in ((0, pl.ds(0, 256)), (1, pl.ds(0, 128))):
+                found = [sums[last(z, b), rows, lanes] for z in range(RING)]
+                for m in range(RING):
+                    some = [value[m * ROWS : (m + 1) * ROWS] for value in found]
+                    yield m, pl.ds(256 * b, lanes.size), jnp.concatenate(some, axis=0)
+            return
+        places = [at(x, a) for x in range(RING)]
+        for b, lanes, to in ((1, pl.ds(128, 128), 0), (2, pl.ds(0, 256), 128)):
+            for m in range(RING):
+                end = last(m, b)
+                some = [sums[end, place_x, lanes] for place_x in places]
+                yield m, pl.ds(to, lanes.size), jnp.concatenate(some, axis=0)
 
     def await_bytes(ref, semaphore):
         pltpu.make_async_copy(ref, ref, semaphore).wait()
@@ -289,7 +293,7 @@
                 a = owner(p, 0, step)
                 pair_copies[k, p, step] = pltpu.make_async_remote_copy(
                     src_ref=outgoing[p].at[k, a], dst_ref=pair[p].at[k, a],
-                    send_sem=sent.at[1], recv_sem=pair_recv.at[k * 4 + n],
+                    send_sem=sent.at[1], recv_sem=pair_recv.at[k * 6 + (p if step == 2 else 2 + n)],
                     device_id=partner, device_id_type=MESH,
                 )
 
@@ -346,9 +350,12 @@
             pair_copies[k, p, step].start()
 
     def join_partner(k, step):
-        await_bytes(msg.at[0, pl.ds(0, 2)], pair_recv.at[k * 4 + STEPS.index(step)])
+        if step != 2:
+            await_bytes(msg.at[0, pl.ds(0, 2)], pair_recv.at[k * 6 + 2 + STEPS.index(step)])
         for p in range(3):
             a = owner(p, 0, step)
+            if step == 2:
+                await_bytes(pair[p].at[k, a], pair_recv.at[k * 6 + p])
             for m, lanes, value in blocks(k, p, a, c):
                 arrived_p = pair[p]
                 arrived_p[k, a, m, :, lanes] = (

time: 49.8 us -> 49.5 us (level)
  no operation moved by 1% of the time
where the time goes in v6:
time: 49.5 us; the launch traced here: 49.3 us
  Pallas kernels  47.1 us (95%)
  local copies, waits for them, and re-layouts  1.47 us (3%)
  between operations  0.66 us (1%)
    pallas_call x1, Pallas kernels, body(): pl.pallas_call(kernel, out_shape=jax.ShapeDtypeStruct((COLS, OWN), BF), i...  47.1 us
    unnamed x1, local copies, waits for them, and re-layouts  1.47 us

profile of v6, /device:TPU:0, one launch (start us, length us, event | category | flops | bytes accessed | tf_op | source)
XLA Modules:
  0.0 49.3 jit_solution(3747160666981780359)
XLA Ops:
  0.7 47.1 %relational_layer.1 = bf16[32,1024]{1,0:T(8,128)(2,1)} custom-call(bf16[32,1024]{1,0:T(8,128)(2,1)} %bitcast.9, bf16[4,512,512]{2,1,0:T(8,128)(2,1)} %rel.1, bf16[512,512]{1,0:T(8,128)(2,1)} %own.1, f32[1,512]{1,0:T(1,128)} %bitcast.10, s32[4,1024]{1,0:T(4,128)} %degree_hbm.1, s32[3,1,64]{2,1,0:T(1,128)} %bitcast.11, s32[1,1]{1,0:T(1,128)S(6)} %copy.10.live, ...), custom_call_target="tpu_custom_call" | custom-call | tf_op jit(solution)/shard_map/relational_layer/pallas_call | solution.py:468
  47.8 1.5 %copy.11 = bf16[1024,32]{0,1:T(8,128)(2,1)} copy(bf16[1024,32]{0,1:T(8,128)(2,1)} %bitcast.8) | data formatting | bytes 131072
